TPU v7x, 256 devices: a whole 4x4x8 slice. The times are simulated.
256 devices in a mesh: dp: 8 (over y, x_hi), centers: 32 (over z, x_lo, core).
Axes of the slice: x: 4 (x_hi: 2, x_lo: 2; x = x_hi * 2 + x_lo), y: 4, z: 8, core: 2. Of those that a mesh axis runs over, the one named last changes fastest.
Arguments:
- points: bfloat16 [32768, 32], P('dp'), may hold values from -6 to 6
- centers: bfloat16 [65536, 32], P('centers'), may hold values from -6 to 6
- coef: bfloat16 [65536, 64], P('centers'), may hold values from -0.09375 to 0.09375
Outputs:
- product: float32 [65536, 64], P('centers')
All inputs are finite; a program needn't handle non-finite values.
Results may differ from a plain program's by a relative error of at most 0.0003.
Values may be sent and summed in bfloat16 or wider, within the bound.
A program may use at most 128 MiB of HBM per device.

v0:
```python
import jax
import jax.numpy as jnp
from jax import lax
from jax.sharding import PartitionSpec as P


def in_blocks(array, dim, length):
    before, after = (array.shape[:dim], array.shape[dim + 1 :])
    return jnp.moveaxis(array.reshape(*before, length, -1, *after), dim, 0)


def sum_at_owner(array, axis, dim):
    parts = in_blocks(array, dim, lax.axis_size(axis))
    arrived = lax.all_to_all(parts, axis, split_axis=0, concat_axis=0, tiled=True)
    return arrived.astype(jnp.float32).sum(axis=0)


def joined_along(parts, dim):
    lengths = list(parts.shape[1:])
    lengths[dim] *= parts.shape[0]
    return jnp.moveaxis(parts, 0, dim).reshape(lengths)


def from_everyone(array, axis):
    length = lax.axis_size(axis)
    return lax.all_to_all(
        jnp.broadcast_to(array[None], (length, *array.shape)), axis, 0, 0, tiled=True
    )


def gather_directly(array, axis, dim):
    return joined_along(from_everyone(array, axis), dim)


def sent_together(arrays, axis, dim, along):
    both = jnp.concatenate(arrays, axis=along)
    filled, at, done = (lax.all_gather(both, axis, axis=dim, tiled=True), 0, [])
    for a in arrays:
        done.append(lax.slice_in_dim(filled, at, at + a.shape[along], axis=along))
        at += a.shape[along]
    return tuple(done)


def of_everyone(array, axis):
    return from_everyone(array, axis).sum(axis=0)


def kernel_block(left_pts, left_sq, right_pts, right_sq, features):
    inner = lax.dot_general(
        left_pts, right_pts, (((1,), (1,)), ((), ())), preferred_element_type=jnp.float32
    )
    dist = left_sq[:, None] + right_sq[None, :] - 2.0 * inner
    return jnp.exp(dist * (-2.0 / features)).astype(jnp.bfloat16)


def squares(values):
    wide = values.astype(jnp.float32)
    return jnp.sum(wide * wide, axis=1)


def on_device(points, centers, coef):
    features = points.shape[1]
    local_pts = points.shape[0]
    local_cen = centers.shape[0]
    outs_count = coef.shape[1]
    block_pts = min(1024, local_pts)
    block_count = local_pts // block_pts
    cen_sq = squares(centers)
    point_blocks = points.reshape(block_count, block_pts, features)
    scalar_zero = jnp.zeros((), jnp.float32)

    def forward_keep(carry, block):
        kernel = kernel_block(block, squares(block), centers, cen_sq, features)
        return (carry, (kernel, jnp.dot(kernel, coef, preferred_element_type=jnp.float32)))

    unused, (tiles, partial_value) = lax.scan(forward_keep, scalar_zero, point_blocks)
    forward_part = partial_value.reshape(local_pts, outs_count)
    shared = sum_at_owner(forward_part.astype(jnp.bfloat16), "centers", 0).astype(jnp.bfloat16)
    forward = gather_directly(shared, "centers", 0)
    forward_blocks = forward.reshape(block_count, block_pts, outs_count)
    back = jnp.einsum("bij,bio->jo", tiles, forward_blocks, preferred_element_type=jnp.float32)
    total_pts = local_pts * lax.axis_size("dp")
    back = back * (1.0 / jnp.sqrt(jnp.float32(total_pts)))
    own_count = local_cen // lax.axis_size("dp")
    own_start = lax.axis_index("dp") * own_count
    own_cen = lax.dynamic_slice_in_dim(centers, own_start, own_count, 0)
    own_sq = squares(own_cen)
    piece_cen, piece_coef = sent_together((centers, coef), "centers", 0, 1)
    kernel = kernel_block(own_cen, own_sq, piece_cen, squares(piece_cen), features)
    regular = jnp.dot(kernel, piece_coef, preferred_element_type=jnp.float32)
    placed = lax.dynamic_update_slice_in_dim(jnp.zeros_like(back), regular, own_start, 0)
    return of_everyone(back + placed, "dp")


def solution(mesh):
    in_specs = (P("dp", None), P("centers", None), P("centers", None))
    out_specs = P("centers", None)
    return jax.shard_map(
        on_device, mesh=mesh, in_specs=in_specs, out_specs=out_specs, check_vma=False
    )
```

profile of v0, /device:TPU:1, one launch (start us, length us, event | category | flops | bytes accessed | tf_op | source)
XLA Modules:
  0.0 208.0 jit_solution(1311128354070534383)
XLA Ops:
  6.5 1.8 pad_maximum_fusion
  8.4 1.4 copy.10
  9.8 1.0 multiply_reduce_fusion.2
  10.8 24.2 %while.12 = (s32[]{:T(128)}, bf16[4,1024,2048]{2,1,0:T(8,128)(2,1)}, bf16[4,1024,64]{1,2,0:T(8,128)(2,1)S(1)}, bf16[4,1024,32]{2,1,0:T(8,128)(2,1)S(1)}, f32[204...) while((s32[]{:T(128)}, bf16[4,1024,2048]{2,1,0:T(8,128)(2,1)}, ...), condition=%wide.region_3.4_spmd, body=%wide.region_1.3_spmd.sunk | while | flops 413236224 | bytes 14632065 | solution.py:76
  11.0 4.4 %bitcast_dynamic-update-slice_fusion.2 = (bf16[4,1024,2048]{2,1,0:T(8,128)(2,1)}, bf16[1024,2048]{1,0:T(8,128)(2,1)S(1)}) fusion(bf16[4,1024,2048]{2,1,0:T(8,128)(2,1)} %get-tuple-element.117, s32[]{:T(128)S(6)} %copy.22, bf16[2048,32]{0,1:T(8,128)(2,1)} %get-tuple-element.129, bf16[4,1024,32]{2,1,0:T(8,128)(2,1)S(1)} %get-tuple-element.127, ...), kind=kOutput, calls=%fused_computation.1.clone.1 | convolution fusion | flops 144703488 | bytes 8795136 | tf_op jit(solution)/shard_map/while/body/eval_jaxpr/dot_general | solution.py:49
  15.4 1.4 fusion.41
  17.0 4.4 %bitcast_dynamic-update-slice_fusion.2 = (bf16[4,1024,2048]{2,1,0:T(8,128)(2,1)}, bf16[1024,2048]{1,0:T(8,128)(2,1)S(1)}) fusion(bf16[4,1024,2048]{2,1,0:T(8,128)(2,1)} %get-tuple-element.117, s32[]{:T(128)S(6)} %copy.22, bf16[2048,32]{0,1:T(8,128)(2,1)} %get-tuple-element.129, bf16[4,1024,32]{2,1,0:T(8,128)(2,1)S(1)} %get-tuple-element.127, ...), kind=kOutput, calls=%fused_computation.1.clone.1 | convolution fusion | flops 144703488 | bytes 8795136 | tf_op jit(solution)/shard_map/while/body/eval_jaxpr/dot_general | solution.py:49
  21.5 1.4 fusion.41
  23.1 4.4 %bitcast_dynamic-update-slice_fusion.2 = (bf16[4,1024,2048]{2,1,0:T(8,128)(2,1)}, bf16[1024,2048]{1,0:T(8,128)(2,1)S(1)}) fusion(bf16[4,1024,2048]{2,1,0:T(8,128)(2,1)} %get-tuple-element.117, s32[]{:T(128)S(6)} %copy.22, bf16[2048,32]{0,1:T(8,128)(2,1)} %get-tuple-element.129, bf16[4,1024,32]{2,1,0:T(8,128)(2,1)S(1)} %get-tuple-element.127, ...), kind=kOutput, calls=%fused_computation.1.clone.1 | convolution fusion | flops 144703488 | bytes 8795136 | tf_op jit(solution)/shard_map/while/body/eval_jaxpr/dot_general | solution.py:49
  27.5 1.4 fusion.41
  29.1 4.4 %bitcast_dynamic-update-slice_fusion.2 = (bf16[4,1024,2048]{2,1,0:T(8,128)(2,1)}, bf16[1024,2048]{1,0:T(8,128)(2,1)S(1)}) fusion(bf16[4,1024,2048]{2,1,0:T(8,128)(2,1)} %get-tuple-element.117, s32[]{:T(128)S(6)} %copy.22, bf16[2048,32]{0,1:T(8,128)(2,1)} %get-tuple-element.129, bf16[4,1024,32]{2,1,0:T(8,128)(2,1)S(1)} %get-tuple-element.127, ...), kind=kOutput, calls=%fused_computation.1.clone.1 | convolution fusion | flops 144703488 | bytes 8795136 | tf_op jit(solution)/shard_map/while/body/eval_jaxpr/dot_general | solution.py:49
  33.5 1.4 fusion.41
  35.8 34.4 %all_to_all.15 = bf16[32,128,64]{1,2,0:T(8,128)(2,1)S(1)} all-to-all(bf16[32,128,64]{1,2,0:T(8,128)(2,1)S(1)} %copy.12), channel_id=1, replica_groups=mesh['dp'=8,'centers'=32] {'centers'}, dimensions={0} | all-to-all | bytes 1048576 | tf_op jit(solution)/shard_map/all_to_all | solution.py:14
  70.2 0.9 broadcast_in_dim.20
  71.1 4.1 %all-to-all-start.1 = ((bf16[32,128,64]{1,2,0:T(8,128)(2,1)}), bf16[32,128,64]{1,2,0:T(8,128)(2,1)S(1)}, u32[]{:S(2)}, u32[]{:S(2)}) async-start(bf16[32,128,64]{1,2,0:T(8,128)(2,1)} %broadcast_in_dim.20), calls=%async_computation.1 | async-start | bytes 1048576 | tf_op jit(solution)/shard_map/all_to_all | solution.py:26
  75.2 0.7 multiply_reduce_fusion.3
  76.0 22.9 %all-to-all-done.1 = bf16[32,128,64]{1,2,0:T(8,128)(2,1)S(1)} async-done(((bf16[32,128,64]{1,2,0:T(8,128)(2,1)}), bf16[32,128,64]{1,2,0:T(8,128)(2,1)S(1)}, u32[]{:S(2)}, u32[]{:S(2)}) %all-to-all-start.1) | async-done | bytes 524320 | tf_op jit(solution)/shard_map/all_to_all | solution.py:26
  99.3 9.1 %fusion.12 = f32[2048,64]{0,1:T(8,128)S(1)} fusion(bf16[4,1024,2048]{2,1,0:T(8,128)(2,1)} %get-tuple-element.43, bf16[4,1024,64]{1,0,2:T(4,128)(2,1)S(1)} %reshape_reshape.3), kind=kOutput, calls=%fused_computation.18 | convolution fusion | flops 1073872896 | bytes 17825792 | tf_op jit(solution)/shard_map/bij,bio->jo/dot_general | solution.py:81
  108.4 7.4 %all-gather.2.cloned.1.call-done = bf16[65536,96]{0,1:T(8,128)(2,1)} async-done(((bf16[2048,96]{0,1:T(8,128)(2,1)}), bf16[65536,96]{0,1:T(8,128)(2,1)}) %all-gather.2.cloned.1.call-update) | async-done | bytes 12582928 | tf_op jit(solution)/shard_map/all_gather | solution.py:37
  115.8 3.4 %multiply_reduce_fusion.1 = f32[65536]{0:T(1024)S(1)} fusion(bf16[65536,96]{0,1:T(8,128)(2,1)} %all-gather.2.cloned.1.call-done), kind=kLoop, calls=%fused_computation.15 | loop fusion | flops 6225920 | bytes 4456448 | tf_op jit(solution)/shard_map/reduce_sum | solution.py:58
  119.2 21.6 %fusion.18 = f32[2048,64]{0,1:T(8,128)S(1)} fusion(f32[2048,64]{0,1:T(8,128)S(1)} %fusion.12, s32[]{:T(128)S(6)} %select_n.4, bf16[65536,96]{0,1:T(8,128)(2,1)} %all-gather.2.cloned.1.call-done, f32[65536]{0:T(1024)S(1)} %multiply_reduce_fusion.1, f32[256]{0:T(256)S(1)} %multiply_reduce_fusion.3, bf16[2048,32]{0,1:T(8,128)(2,1)} %get-tuple-element.137), kind=kOutput, calls=%fused_computation.20 | convolution fusion | flops 3305127936 | bytes 12994560 | tf_op jit(solution)/shard_map/dot_general | solution.py:90
  140.8 0.5 broadcast_in_dim.34
  141.4 56.5 %all_to_all.16 = f32[8,2048,64]{1,2,0:T(8,128)} all-to-all(f32[8,2048,64]{1,2,0:T(8,128)S(1)} %broadcast_in_dim.34), channel_id=1, replica_groups=mesh['dp'=8,'centers'=32] {'dp'}, dimensions={0} | all-to-all | bytes 8388608 | tf_op jit(solution)/shard_map/all_to_all | solution.py:26
  197.9 3.3 %reduce_sum.61 = f32[2048,64]{0,1:T(8,128)} reduce(f32[8,2048,64]{1,2,0:T(8,128)} %all_to_all.16, f32[]{:T(128)} %constant.16.clone.1), dimensions={0}, to_apply=%region_7.8 | reduce | flops 917504 | bytes 4718596 | tf_op jit(solution)/shard_map/reduce_sum | solution.py:45
  (22 shorter events, 2.3 us)
Async XLA Ops:
  6.5 109.2 %all-gather.2.cloned.1.call-start = ((), (), s32[]{:S(2)}) async-start(), calls=%async_computation.3 | async-start | bytes 12976128 | tf_op jit(solution)/shard_map/all_gather | solution.py:37
  10.8 4.6 %copy-start = (bf16[2048,64]{0,1:T(8,128)(2,1)S(1)}, bf16[2048,64]{0,1:T(8,128)(2,1)}, u32[]{:S(2)}) copy-start(bf16[2048,64]{0,1:T(8,128)(2,1)} %get-tuple-element.130) | copy-start | bytes 786436 | tf_op jit(solution)/shard_map/while
  16.8 4.7 %copy-start = (bf16[2048,64]{0,1:T(8,128)(2,1)S(1)}, bf16[2048,64]{0,1:T(8,128)(2,1)}, u32[]{:S(2)}) copy-start(bf16[2048,64]{0,1:T(8,128)(2,1)} %get-tuple-element.130) | copy-start | bytes 786436 | tf_op jit(solution)/shard_map/while
  22.9 4.6 %copy-start = (bf16[2048,64]{0,1:T(8,128)(2,1)S(1)}, bf16[2048,64]{0,1:T(8,128)(2,1)}, u32[]{:S(2)}) copy-start(bf16[2048,64]{0,1:T(8,128)(2,1)} %get-tuple-element.130) | copy-start | bytes 786436 | tf_op jit(solution)/shard_map/while
  28.9 4.7 %copy-start = (bf16[2048,64]{0,1:T(8,128)(2,1)S(1)}, bf16[2048,64]{0,1:T(8,128)(2,1)}, u32[]{:S(2)}) copy-start(bf16[2048,64]{0,1:T(8,128)(2,1)} %get-tuple-element.130) | copy-start | bytes 786436 | tf_op jit(solution)/shard_map/while
  71.1 27.7 %all-to-all-start.1 = ((bf16[32,128,64]{1,2,0:T(8,128)(2,1)}), bf16[32,128,64]{1,2,0:T(8,128)(2,1)S(1)}, u32[]{:S(2)}, u32[]{:S(2)}) async-start(bf16[32,128,64]{1,2,0:T(8,128)(2,1)} %broadcast_in_dim.20), calls=%async_computation.1 | async-start | bytes 1048576 | tf_op jit(solution)/shard_map/all_to_all | solution.py:26
Sparse Core Ops, SparseCore 0:
  9.2 106.5 all-gather.1
where the time goes:
time: 209 us; the launch traced here: 208 us
  blocking collectives  90.9 us (43%)
  matrix products  53.9 us (26%)
  waiting for transfers between devices  30.2 us (14%)
  between operations  13.5 us (6%)
  other arithmetic  11.1 us (5%)
  local copies, waits for them, and re-layouts  4.14 us (2%)
  starting transfers between devices  4.09 us (2%)
    all_to_all x1, blocking collectives, from_everyone(): lax.all_to_all(jnp.broadcast_to(array[None], (length, *array.shape)), axi...  56.5 us
    all_to_all x1, blocking collectives, sum_at_owner(): lax.all_to_all(parts, axis, split_axis=0, concat_axis=0, tiled=True)  34.4 us
    all_to_all x1, waiting for transfers between devices, from_everyone(): lax.all_to_all(jnp.broadcast_to(array[None], (length, *array.shape)), axi...  22.9 us
    dot_general x1, matrix products, on_device(): regular = jnp.dot(kernel, piece_coef, preferred_element_type=jnp.float32)  21.6 us
    dot_general x4, matrix products, kernel_block(): lax.dot_general(left_pts, right_pts, (((1,), (1,)), ((), ())), preferred_...  17.6 us
    dot_general x1, matrix products, on_device(): jnp.einsum('bij,bio->jo', tiles, forward_blocks, preferred_element_type=j...  9.11 us
    all_gather x1, waiting for transfers between devices, sent_together(): filled, at, done = (lax.all_gather(both, axis, axis=dim, tiled=True), 0, [])  7.36 us
    reduce_sum x7, other arithmetic, squares(): return jnp.sum(wide * wide, axis=1)  5.97 us
  transfers between devices with their start and end apart: 2, of which 2 were waited for; matrix products, arithmetic and copies ran while one was open for 19% of the time, Pallas kernels for 0%

commit v1 on v0

v1 whole, which is shorter than its diff:
```python
import math

import jax
import jax.numpy as jnp
import numpy as np
from jax import lax
from jax.experimental import pallas as pl
from jax.experimental.pallas import tpu as pltpu
from jax.sharding import PartitionSpec as P

F32, BF16 = jnp.float32, jnp.bfloat16
MESH = pl.DeviceIdType.MESH
ROWS = 128
TILE = 256
CHUNKS = 2


def split3(x):
    a = x.astype(BF16)
    r = x - a.astype(F32)
    b = r.astype(BF16)
    return a, b, (r - b.astype(F32)).astype(BF16)


def tail_rows(pieces, first, ones):
    n = pieces[0].shape[1]
    row = lax.broadcasted_iota(jnp.int32, (32, n), 0)
    out = jnp.where((row >= ones) & (row < ones + 3), 1.0, 0.0)
    for k, piece in enumerate(pieces):
        out = jnp.where(row == first + k, piece.astype(F32), out)
    return out.astype(BF16)


def fill(dst, feats, scale, scaled, cols):
    wide = feats.astype(F32)
    squares = split3(-scale * jnp.sum(wide * wide, axis=0, keepdims=True))
    parts = split3((2.0 * scale) * wide) if scaled else (feats,) * 3
    for k in range(3):
        dst[32 * k : 32 * (k + 1), cols] = parts[k]
    dst[96:128, cols] = tail_rows(squares, 3 if scaled else 0, 0 if scaled else 3)


def dot(a, b):
    return jnp.dot(a, b, preferred_element_type=F32)


def dot_nt(a, b):
    return lax.dot_general(a, b, (((1,), (1,)), ((), ())), preferred_element_type=F32)


def kernel(
    feats, outs, n_pts, n_cen, total_pts,
    p_ref, z_ref, out_ref,
    bpts, bown, arow, kt, fpart, zslots, zaug, mmacc, fwd,
    sbuf, dbuf, rsend, rrecv, dsend, drecv, outt,
    a_send, a_recv, d1_send, d1_recv, rs_send, rs_recv, ag_send, ag_recv,
    d2_send, d2_recv, ds_send, ds_recv, dg_send, dg_recv,
):
    scale = math.log2(math.e) * 2.0 / feats
    norm = float(np.float32(1.0) / np.sqrt(np.float32(total_pts)))
    d, c = lax.axis_index("dp"), lax.axis_index("centers")
    core, x_lo, z = c % 2, (c // 2) % 2, c // 4
    chip = c // 2
    y, x_hi = d // 2, d % 2
    half = outs // 2
    r_own = pl.multiple_of(half * core, half)
    r_other = pl.multiple_of(half * (1 - core), half)
    cpts = n_pts // CHUNKS
    share = cpts // 16
    dshare = n_cen // 8

    def at(dp, cen):
        return {"dp": dp, "centers": cen}

    partner = at(d, chip * 2 + 1 - core)
    x_next = at(d, z * 4 + (1 - x_lo) * 2 + core)

    def chip_peer(k):
        return (chip + k) % 16

    def group(k):
        return at(d, chip_peer(k) * 2 + core)

    def dp_peer(k):
        return (d + k) % 8

    def remote(src, dst, send, recv, dev):
        return pltpu.make_async_remote_copy(
            src_ref=src, dst_ref=dst, send_sem=send, recv_sem=recv, device_id=dev, device_id_type=MESH
        )

    barrier = pltpu.get_barrier_semaphore()
    for k in range(1, 16):
        pl.semaphore_signal(barrier, inc=1, device_id=group(k), device_id_type=MESH)
    pl.semaphore_signal(barrier, inc=1, device_id=partner, device_id_type=MESH)
    for k in range(1, 8):
        pl.semaphore_signal(barrier, inc=1, device_id=at(dp_peer(k), c), device_id_type=MESH)

    def prep_own(t, _):
        cols = pl.ds(pl.multiple_of(t * TILE, TILE), TILE)
        fill(bown, z_ref[0:feats, cols], scale, True, cols)
        arow[cols, :] = bown[:, cols].T
        return 0

    lax.fori_loop(0, n_cen // TILE, prep_own, 0)
    pl.semaphore_wait(barrier, 23)

    dz = (y + 4 * ((x_hi + core) % 2)) % 8
    a0 = remote(z_ref, zslots.at[0], a_send.at[0], a_recv.at[0], at(d, ((z + 8 - dz) % 8) * 4 + x_lo * 2 + core))
    a0_local = pltpu.make_async_copy(z_ref, zslots.at[0], a_recv.at[0])
    a1 = remote(zslots.at[0], zslots.at[1], a_send.at[1], a_recv.at[1], x_next)
    a2 = remote(zslots.at[0], zslots.at[2], a_send.at[2], a_recv.at[2], partner)
    a3 = remote(zslots.at[1], zslots.at[3], a_send.at[3], a_recv.at[3], partner)

    @pl.when(dz != 0)
    def _():
        a0.start()

    @pl.when(dz == 0)
    def _():
        a0_local.start()

    def prep_pts(t, _):
        cols = pl.ds(pl.multiple_of(t * 512, 512), 512)
        fill(bpts, p_ref[:, cols], scale, False, cols)
        return 0

    lax.fori_loop(0, n_pts // 512, prep_pts, 0)

    def nm_step(t, _):
        cols = pl.ds(pl.multiple_of(t * TILE, TILE), TILE)
        right = bpts[:, cols]
        acc = None
        for b in range(n_cen // TILE):
            rows = pl.ds(b * TILE, TILE)
            tile = jnp.exp2(dot(arow[rows, :], right)).astype(BF16)
            kt[rows, cols] = tile
            one = dot(z_ref[feats : feats + outs, rows], tile)
            acc = one if acc is None else acc + one
        fpart[:, cols] = acc
        return 0

    def d1(q):
        return remote(sbuf.at[q], dbuf.at[q], d1_send.at[q], d1_recv.at[q], partner)

    def d1_go(q):
        sbuf[q] = fpart[pl.ds(r_other, half), q * cpts : (q + 1) * cpts].astype(BF16)
        d1(q).start()

    def rs(q, k):
        lanes = pl.ds(pl.multiple_of(chip_peer(k) * share, share), share)
        return remote(rsend.at[q, :, lanes], rrecv.at[q, k], rs_send.at[q, k], rs_recv.at[q, k], group(k))

    def rs_go(q):
        d1(q).wait_recv()
        mine = fpart[pl.ds(r_own, half), q * cpts : (q + 1) * cpts]
        rsend[q] = (mine + dbuf[q].astype(F32)).astype(BF16)
        for k in range(1, 16):
            rs(q, k).start()

    own_rows = pl.ds(r_own, half)

    def ag(q, k):
        where = fwd.at[own_rows, pl.ds(pl.multiple_of(q * cpts + chip * share, share), share)]
        return remote(where, where, ag_send.at[q, k], ag_recv.at[q, k], group(k))

    def ag_go(q):
        total = rsend[q, :, pl.ds(pl.multiple_of(chip * share, share), share)].astype(F32)
        for k in range(1, 16):
            rs(q, k).wait_recv()
            total = total + rrecv[q, k].astype(F32)
        fwd[own_rows, pl.ds(pl.multiple_of(q * cpts + chip * share, share), share)] = total.astype(BF16)
        for k in range(1, 16):
            ag(q, k).start()

    def d2(q):
        where = fwd.at[own_rows, q * cpts : (q + 1) * cpts]
        return remote(where, where, d2_send.at[q], d2_recv.at[q], partner)

    def d2_go(q):
        for k in range(1, 16):
            ag(q, k).wait_recv()
        d2(q).start()

    steps = n_pts // TILE // 4
    lax.fori_loop(0, 2 * steps, nm_step, 0)
    d1_go(0)
    lax.fori_loop(2 * steps, 3 * steps, nm_step, 0)
    rs_go(0)
    lax.fori_loop(3 * steps, 4 * steps, nm_step, 0)
    d1_go(1)

    mmacc[...] = jnp.zeros_like(mmacc)

    def mm_prep(slot):
        def step(t, _):
            cols = pl.ds(pl.multiple_of(t * 512, 512), 512)
            fill(zaug, zslots[slot, 0:feats, cols], scale, False, cols)
            return 0

        lax.fori_loop(0, n_cen // 512, step, 0)

    def mm(slot, lo, hi):
        def step(t, _):
            rows = pl.ds(pl.multiple_of(t * TILE, TILE), TILE)
            left = zaug[:, rows].T
            weights = zslots[slot, feats : feats + outs, rows]
            for b in range(n_cen // TILE):
                cols = pl.ds(b * TILE, TILE)
                tile = jnp.exp2(dot(left, bown[:, cols])).astype(BF16)
                mmacc[:, cols] += dot(weights, tile)
            return 0

        lax.fori_loop(lo, hi, step, 0)

    blocks = n_cen // TILE
    a0_local.wait()
    a1.start()
    a2.start()
    mm_prep(0)
    mm(0, 0, blocks // 2)
    rs_go(1)
    mm(0, blocks // 2, blocks)
    ag_go(0)
    a2.wait_recv()
    mm_prep(2)
    mm(2, 0, blocks)
    ag_go(1)
    a1.wait_recv()
    a3.start()
    mm_prep(1)
    mm(1, 0, blocks)
    d2_go(0)
    a3.wait_recv()
    mm_prep(3)
    mm(3, 0, blocks)
    d2_go(1)
    d2(0).wait_recv()
    d2(1).wait_recv()

    def back(k):
        rows = pl.ds(pl.multiple_of(dp_peer(k) * dshare, dshare), dshare)
        return dot_nt(fwd[...], kt[rows, :]) * norm + mmacc[:, rows]

    def ds_copy(k):
        return remote(dsend.at[k], drecv.at[k], ds_send.at[k], ds_recv.at[k], at(dp_peer(k), c))

    def back_step(k, _):
        dsend[k] = back(k)
        ds_copy(k).start()
        return 0

    lax.fori_loop(1, 8, back_step, 0)
    total = back(0)
    for k in range(1, 8):
        ds_copy(k).wait_recv()
        total = total + drecv[k]
    mine = pl.ds(pl.multiple_of(d * dshare, dshare), dshare)
    outt[:, mine] = total

    def dg(k):
        return remote(outt.at[:, mine], outt.at[:, mine], dg_send.at[k], dg_recv.at[k], at(dp_peer(k), c))

    for k in range(1, 8):
        dg(k).start()

    @pl.when(dz != 0)
    def _():
        a0.wait_send()

    for copy in (a1, a2, a3):
        copy.wait_send()
    for q in range(CHUNKS):
        d1(q).wait_send()
        d2(q).wait_send()
        for k in range(1, 16):
            rs(q, k).wait_send()
            ag(q, k).wait_send()
    for k in range(1, 8):
        ds_copy(k).wait_send()
    for k in range(1, 8):
        dg(k).wait_recv()
    out_ref[...] = outt[...].T
    for k in range(1, 8):
        dg(k).wait_send()


def solution(mesh):
    def on_device(points, centers, coef):
        n_pts, feats = points.shape
        n_cen, outs = coef.shape
        cpts = n_pts // CHUNKS
        dma = pltpu.SemaphoreType.DMA
        stacked = jnp.concatenate((centers, coef), axis=1).T

        def body(*refs):
            kernel(feats, outs, n_pts, n_cen, n_pts * 8, *refs)

        return pl.pallas_call(
            body,
            out_shape=jax.ShapeDtypeStruct((n_cen, outs), F32),
            in_specs=[pl.BlockSpec(memory_space=pltpu.VMEM)] * 2,
            out_specs=pl.BlockSpec(memory_space=pltpu.VMEM),
            scratch_shapes=[
                pltpu.VMEM((ROWS, n_pts), BF16),
                pltpu.VMEM((ROWS, n_cen), BF16),
                pltpu.VMEM((n_cen, ROWS), BF16),
                pltpu.VMEM((n_cen, n_pts), BF16),
                pltpu.VMEM((outs, n_pts), F32),
                pltpu.VMEM((4, feats + outs, n_cen), BF16),
                pltpu.VMEM((ROWS, n_cen), BF16),
                pltpu.VMEM((outs, n_cen), F32),
                pltpu.VMEM((outs, n_pts), BF16),
                pltpu.VMEM((CHUNKS, outs // 2, cpts), BF16),
                pltpu.VMEM((CHUNKS, outs // 2, cpts), BF16),
                pltpu.VMEM((CHUNKS, outs // 2, cpts), BF16),
                pltpu.VMEM((CHUNKS, 16, outs // 2, cpts // 16), BF16),
                pltpu.VMEM((8, outs, n_cen // 8), F32),
                pltpu.VMEM((8, outs, n_cen // 8), F32),
                pltpu.VMEM((outs, n_cen), F32),
                dma((4,)), dma((4,)),
                dma((CHUNKS,)), dma((CHUNKS,)),
                dma((CHUNKS, 16)), dma((CHUNKS, 16)),
                dma((CHUNKS, 16)), dma((CHUNKS, 16)),
                dma((CHUNKS,)), dma((CHUNKS,)),
                dma((8,)), dma((8,)),
                dma((8,)), dma((8,)),
            ],
            compiler_params=pltpu.CompilerParams(
                collective_id=0, has_side_effects=True, vmem_limit_bytes=60 * 1024 * 1024
            ),
        )(points.T, stacked)

    in_specs = (P("dp", None), P("centers", None), P("centers", None))
    return jax.shard_map(
        on_device, mesh=mesh, in_specs=in_specs, out_specs=P("centers", None), check_vma=False
    )
```

time: 209 us -> 115 us (0.55)
  Pallas kernels: 0 us -> 111 us
  blocking collectives: 90.9 us -> 0 us
  matrix products: 53.9 us -> 0 us
  waiting for transfers between devices: 30.2 us -> 0 us
  between operations: 13.5 us -> 0.01 us
  other arithmetic: 11.1 us -> 1.75 us
  starting transfers between devices: 4.09 us -> 0 us
    pallas_call x0 -> x1, Pallas kernels: none -> 111 us  [on_device(): pl.pallas_call(body, out_shape=jax.ShapeDtypeStruct((n_cen, outs), F32),...]
    all_to_all x2 -> x0, blocking collectives: 90.9 us -> none  [the longest x1 56.5 us: from_everyone(): lax.all_to_all(jnp.broadcast_to(array[None], (length, *array.shape)), axi...]
    dot_general x10 -> x0, matrix products: 53.9 us -> none  [the longest x1 21.6 us: on_device(): regular = jnp.dot(kernel, piece_coef, preferred_element_type=jnp.float32)]
    all_to_all x1 -> x0, waiting for transfers between devices: 22.9 us -> none  [from_everyone(): lax.all_to_all(jnp.broadcast_to(array[None], (length, *array.shape)), axi...]
    reduce_sum x9 -> x0, other arithmetic: 9.33 us -> none  [the longest x7 5.97 us: squares(): return jnp.sum(wide * wide, axis=1)]
    all_gather x1 -> x0, waiting for transfers between devices: 7.36 us -> none  [sent_together(): filled, at, done = (lax.all_gather(both, axis, axis=dim, tiled=True), 0, [])]
    all_to_all x1 -> x0, starting transfers between devices: 4.09 us -> none  [from_everyone(): lax.all_to_all(jnp.broadcast_to(array[None], (length, *array.shape)), axi...]
    pallas_call x0 -> x1, local copies, waits for them, and re-layouts: none -> 2.34 us  [on_device(): pl.pallas_call(body, out_shape=jax.ShapeDtypeStruct((n_cen, outs), F32),...]
  transfers between devices with their start and end apart: 2 -> 0, of which waited for: 2 -> 0; matrix products, arithmetic and copies ran while one was open for 19% -> 0% of each run, Pallas kernels for 0% -> 0%
where the time goes in v1:
time: 115 us
  Pallas kernels  111 us (97%)
  local copies, waits for them, and re-layouts  2.34 us (2%)
  other arithmetic  1.75 us (2%)
    pallas_call x1, Pallas kernels, on_device(): pl.pallas_call(body, out_shape=jax.ShapeDtypeStruct((n_cen, outs), F32),...  111 us
    pallas_call x1, local copies, waits for them, and re-layouts, on_device(): pl.pallas_call(body, out_shape=jax.ShapeDtypeStruct((n_cen, outs), F32),...  2.34 us

profile of v1, /device:TPU:1, one launch (start us, length us, event | category | flops | bytes accessed | tf_op | source)
XLA Modules:
  0.0 114.7 jit_solution(4479941041641359725)
XLA Ops:
  0.0 1.8 %maximum_bitcast_fusion.refs_1_ = bf16[96,2048]{1,0:T(8,128)(2,1)} fusion(bf16[2048,64]{0,1:T(8,128)(2,1)} %param.5, bf16[2048,32]{0,1:T(8,128)(2,1)} %param.4), kind=kLoop, calls=%fused_computation | loop fusion | flops 786432 | bytes 786432 | tf_op jit(solution)/shard_map/transpose | solution.py:294
  1.8 110.6 %shard_map.37 = f32[2048,64]{1,0:T(8,128)} custom-call(bf16[32,4096]{1,0:T(8,128)(2,1)} %bitcast.3, bf16[96,2048]{1,0:T(8,128)(2,1)} %maximum_bitcast_fusion.refs_1_), custom_call_target="tpu_custom_call" | custom-call | tf_op jit(solution)/shard_map/pallas_call | solution.py:299
  112.4 2.3 %copy.4 = f32[2048,64]{0,1:T(8,128)} copy(f32[2048,64]{1,0:T(8,128)} %shard_map.37) | data formatting | bytes 1048576 | tf_op jit(solution)/shard_map/pallas_call | solution.py:299

commit v2 on v1

--- a/solution.py
+++ b/solution.py
@@ -12,6 +12,7 @@
 MESH = pl.DeviceIdType.MESH
 ROWS = 128
 TILE = 256
+WIDE = 512
 CHUNKS = 2
 
 
@@ -51,7 +52,7 @@
 def kernel(
     feats, outs, n_pts, n_cen, total_pts,
     p_ref, z_ref, out_ref,
-    bpts, bown, arow, kt, fpart, zslots, zaug, mmacc, fwd,
+    bpts, bown, arow, kt, tiles, fpart, zslots, zaug, mmacc, fwd,
     sbuf, dbuf, rsend, rrecv, dsend, drecv, outt,
     a_send, a_recv, d1_send, d1_recv, rs_send, rs_recv, ag_send, ag_recv,
     d2_send, d2_recv, ds_send, ds_recv, dg_send, dg_recv,
@@ -102,15 +103,17 @@
         arow[cols, :] = bown[:, cols].T
         return 0
 
-    lax.fori_loop(0, n_cen // TILE, prep_own, 0)
-    pl.semaphore_wait(barrier, 23)
+    with jax.named_scope("prep_own"):
+        lax.fori_loop(0, n_cen // TILE, prep_own, 0)
+    with jax.named_scope("barrier"):
+        pl.semaphore_wait(barrier, 23)
 
     dz = (y + 4 * ((x_hi + core) % 2)) % 8
     a0 = remote(z_ref, zslots.at[0], a_send.at[0], a_recv.at[0], at(d, ((z + 8 - dz) % 8) * 4 + x_lo * 2 + core))
     a0_local = pltpu.make_async_copy(z_ref, zslots.at[0], a_recv.at[0])
-    a1 = remote(zslots.at[0], zslots.at[1], a_send.at[1], a_recv.at[1], x_next)
-    a2 = remote(zslots.at[0], zslots.at[2], a_send.at[2], a_recv.at[2], partner)
-    a3 = remote(zslots.at[1], zslots.at[3], a_send.at[3], a_recv.at[3], partner)
+    a1 = remote(zslots.at[0], zslots.at[1], a_send.at[1], a_recv.at[1], partner)
+    a2 = remote(zslots.at[0], zslots.at[2], a_send.at[2], a_recv.at[2], x_next)
+    a3 = remote(zslots.at[2], zslots.at[3], a_send.at[3], a_recv.at[3], partner)
 
     @pl.when(dz != 0)
     def _():
@@ -125,19 +128,23 @@
         fill(bpts, p_ref[:, cols], scale, False, cols)
         return 0
 
-    lax.fori_loop(0, n_pts // 512, prep_pts, 0)
-
-    def nm_step(t, _):
-        cols = pl.ds(pl.multiple_of(t * TILE, TILE), TILE)
+    with jax.named_scope("prep_pts"):
+        lax.fori_loop(0, n_pts // 512, prep_pts, 0)
+
+    def nm_tiles(t):
+        cols = pl.ds(pl.multiple_of(t * WIDE, WIDE), WIDE)
         right = bpts[:, cols]
-        acc = None
         for b in range(n_cen // TILE):
             rows = pl.ds(b * TILE, TILE)
-            tile = jnp.exp2(dot(arow[rows, :], right)).astype(BF16)
-            kt[rows, cols] = tile
-            one = dot(z_ref[feats : feats + outs, rows], tile)
-            acc = one if acc is None else acc + one
-        fpart[:, cols] = acc
+            kt[rows, cols] = jnp.exp2(dot(arow[rows, :], right)).astype(BF16)
+
+    def nm_sum(t):
+        cols = pl.ds(pl.multiple_of(t * WIDE, WIDE), WIDE)
+        fpart[:, cols] = dot(z_ref[feats : feats + outs, :], kt[:, cols])
+
+    def nm_step(t, _):
+        nm_sum(t - 1)
+        nm_tiles(t)
         return 0
 
     def d1(q):
@@ -182,15 +189,24 @@
             ag(q, k).wait_recv()
         d2(q).start()
 
-    steps = n_pts // TILE // 4
-    lax.fori_loop(0, 2 * steps, nm_step, 0)
-    d1_go(0)
-    lax.fori_loop(2 * steps, 3 * steps, nm_step, 0)
-    rs_go(0)
-    lax.fori_loop(3 * steps, 4 * steps, nm_step, 0)
-    d1_go(1)
+    steps = n_pts // WIDE
+    with jax.named_scope("nm_a"):
+        nm_tiles(0)
+        lax.fori_loop(1, steps // 2 + 1, nm_step, 0)
+    with jax.named_scope("d1_0"):
+        d1_go(0)
+    with jax.named_scope("nm_b"):
+        lax.fori_loop(steps // 2 + 1, steps * 3 // 4, nm_step, 0)
+    with jax.named_scope("rs_0"):
+        rs_go(0)
+    with jax.named_scope("nm_c"):
+        lax.fori_loop(steps * 3 // 4, steps, nm_step, 0)
+        nm_sum(steps - 1)
+    with jax.named_scope("d1_1"):
+        d1_go(1)
 
     mmacc[...] = jnp.zeros_like(mmacc)
+    blocks = n_cen // WIDE
 
     def mm_prep(slot):
         def step(t, _):
@@ -200,43 +216,67 @@
 
         lax.fori_loop(0, n_cen // 512, step, 0)
 
-    def mm(slot, lo, hi):
-        def step(t, _):
-            rows = pl.ds(pl.multiple_of(t * TILE, TILE), TILE)
-            left = zaug[:, rows].T
-            weights = zslots[slot, feats : feats + outs, rows]
-            for b in range(n_cen // TILE):
-                cols = pl.ds(b * TILE, TILE)
-                tile = jnp.exp2(dot(left, bown[:, cols])).astype(BF16)
-                mmacc[:, cols] += dot(weights, tile)
-            return 0
-
-        lax.fori_loop(lo, hi, step, 0)
-
-    blocks = n_cen // TILE
-    a0_local.wait()
+    def mm_tiles(g):
+        left = zaug[:, pl.ds(pl.multiple_of((g % blocks) * WIDE, WIDE), WIDE)].T
+        for b in range(n_cen // TILE):
+            cols = pl.ds(b * TILE, TILE)
+            tiles[g % 2, :, cols] = jnp.exp2(dot(left, bown[:, cols])).astype(BF16)
+
+    def mm_sum(g):
+        rows = pl.ds(pl.multiple_of((g % blocks) * WIDE, WIDE), WIDE)
+        weights = zslots[g // blocks, feats : feats + outs, rows]
+        for b in range(n_cen // TILE):
+            cols = pl.ds(b * TILE, TILE)
+            mmacc[:, cols] += dot(weights, tiles[g % 2, :, cols])
+
+    def mm_step(g, _):
+        mm_sum(g - 1)
+        mm_tiles(g)
+        return 0
+
+    def mm(lo, hi):
+        lax.fori_loop(lo, hi, mm_step, 0)
+
+    with jax.named_scope("a0_wait"):
+        a0_local.wait()
     a1.start()
     a2.start()
-    mm_prep(0)
-    mm(0, 0, blocks // 2)
-    rs_go(1)
-    mm(0, blocks // 2, blocks)
-    ag_go(0)
-    a2.wait_recv()
-    mm_prep(2)
-    mm(2, 0, blocks)
-    ag_go(1)
-    a1.wait_recv()
+    with jax.named_scope("mm_a"):
+        mm_prep(0)
+        mm_tiles(0)
+        mm(1, blocks // 2)
+    with jax.named_scope("rs_1"):
+        rs_go(1)
+    with jax.named_scope("mm_b"):
+        mm(blocks // 2, blocks)
+    with jax.named_scope("ag_0"):
+        ag_go(0)
+    with jax.named_scope("a1_wait"):
+        a1.wait_recv()
+    with jax.named_scope("mm_c"):
+        mm_prep(1)
+        mm(blocks, 2 * blocks)
+    with jax.named_scope("ag_1"):
+        ag_go(1)
+    with jax.named_scope("a2_wait"):
+        a2.wait_recv()
     a3.start()
-    mm_prep(1)
-    mm(1, 0, blocks)
-    d2_go(0)
-    a3.wait_recv()
-    mm_prep(3)
-    mm(3, 0, blocks)
-    d2_go(1)
-    d2(0).wait_recv()
-    d2(1).wait_recv()
+    with jax.named_scope("mm_d"):
+        mm_prep(2)
+        mm(2 * blocks, 3 * blocks)
+    with jax.named_scope("d2_0"):
+        d2_go(0)
+    with jax.named_scope("a3_wait"):
+        a3.wait_recv()
+    with jax.named_scope("mm_e"):
+        mm_prep(3)
+        mm(3 * blocks, 4 * blocks)
+        mm_sum(4 * blocks - 1)
+    with jax.named_scope("d2_1"):
+        d2_go(1)
+    with jax.named_scope("d2_wait"):
+        d2(0).wait_recv()
+        d2(1).wait_recv()
 
     def back(k):
         rows = pl.ds(pl.multiple_of(dp_peer(k) * dshare, dshare), dshare)
@@ -250,11 +290,13 @@
         ds_copy(k).start()
         return 0
 
-    lax.fori_loop(1, 8, back_step, 0)
-    total = back(0)
-    for k in range(1, 8):
-        ds_copy(k).wait_recv()
-        total = total + drecv[k]
+    with jax.named_scope("back"):
+        lax.fori_loop(1, 8, back_step, 0)
+    with jax.named_scope("back0_dswait"):
+        total = back(0)
+        for k in range(1, 8):
+            ds_copy(k).wait_recv()
+            total = total + drecv[k]
     mine = pl.ds(pl.multiple_of(d * dshare, dshare), dshare)
     outt[:, mine] = total
 
@@ -278,9 +320,10 @@
             ag(q, k).wait_send()
     for k in range(1, 8):
         ds_copy(k).wait_send()
-    for k in range(1, 8):
-        dg(k).wait_recv()
-    out_ref[...] = outt[...].T
+    with jax.named_scope("dg_wait_out"):
+        for k in range(1, 8):
+            dg(k).wait_recv()
+        out_ref[...] = outt[...].T
     for k in range(1, 8):
         dg(k).wait_send()
 
@@ -306,6 +349,7 @@
                 pltpu.VMEM((ROWS, n_cen), BF16),
                 pltpu.VMEM((n_cen, ROWS), BF16),
                 pltpu.VMEM((n_cen, n_pts), BF16),
+                pltpu.VMEM((2, WIDE, n_cen), BF16),
                 pltpu.VMEM((outs, n_pts), F32),
                 pltpu.VMEM((4, feats + outs, n_cen), BF16),
                 pltpu.VMEM((ROWS, n_cen), BF16),

time: 115 us -> 75.9 us (0.66)
  Pallas kernels: 111 us -> 71.7 us
    pallas_call x1, Pallas kernels: 111 us -> 71.7 us  [on_device(): pl.pallas_call(body, out_shape=jax.ShapeDtypeStruct((n_cen, outs), F32),...]
where the time goes in v2:
time: 75.9 us; the launch traced here: 75.8 us
  Pallas kernels  71.7 us (94%)
  local copies, waits for them, and re-layouts  2.34 us (3%)
  other arithmetic  1.75 us (2%)
    pallas_call x1, Pallas kernels, on_device(): pl.pallas_call(body, out_shape=jax.ShapeDtypeStruct((n_cen, outs), F32),...  71.7 us
    pallas_call x1, local copies, waits for them, and re-layouts, on_device(): pl.pallas_call(body, out_shape=jax.ShapeDtypeStruct((n_cen, outs), F32),...  2.34 us
    transpose x1, other arithmetic, on_device(): stacked = jnp.concatenate((centers, coef), axis=1).T  1.75 us

profile of v2, /device:TPU:1, one launch (start us, length us, event | category | flops | bytes accessed | tf_op | source)
XLA Modules:
  0.0 75.8 jit_solution(2626737047461043467)
XLA Ops:
  0.0 1.8 %maximum_bitcast_fusion.refs_1_ = bf16[96,2048]{1,0:T(8,128)(2,1)} fusion(bf16[2048,64]{0,1:T(8,128)(2,1)} %param.5, bf16[2048,32]{0,1:T(8,128)(2,1)} %param.4), kind=kLoop, calls=%fused_computation | loop fusion | flops 786432 | bytes 786432 | tf_op jit(solution)/shard_map/transpose | solution.py:337
  1.8 71.7 %shard_map.37 = f32[2048,64]{1,0:T(8,128)} custom-call(bf16[32,4096]{1,0:T(8,128)(2,1)} %bitcast.3, bf16[96,2048]{1,0:T(8,128)(2,1)} %maximum_bitcast_fusion.refs_1_), custom_call_target="tpu_custom_call" | custom-call | tf_op jit(solution)/shard_map/pallas_call | solution.py:342
  73.4 2.3 %copy.4 = f32[2048,64]{0,1:T(8,128)} copy(f32[2048,64]{1,0:T(8,128)} %shard_map.37) | data formatting | bytes 1048576 | tf_op jit(solution)/shard_map/pallas_call | solution.py:342

commit v3 on v2

v3 whole, which is shorter than its diff:
```python
import math

import jax
import jax.numpy as jnp
import numpy as np
from jax import lax
from jax.experimental import pallas as pl
from jax.experimental.pallas import tpu as pltpu
from jax.sharding import PartitionSpec as P

F32, BF16 = jnp.float32, jnp.bfloat16
MESH = pl.DeviceIdType.MESH
ROWS = 128
TILE = 256
WIDE = 512
CHUNKS = 2


def split3(x):
    a = x.astype(BF16)
    r = x - a.astype(F32)
    b = r.astype(BF16)
    return a, b, (r - b.astype(F32)).astype(BF16)


def tail_rows(pieces, first, ones):
    n = pieces[0].shape[1]
    row = lax.broadcasted_iota(jnp.int32, (32, n), 0)
    out = jnp.where((row >= ones) & (row < ones + 3), 1.0, 0.0)
    for k, piece in enumerate(pieces):
        out = jnp.where(row == first + k, piece.astype(F32), out)
    return out.astype(BF16)


def fill(dst, feats, scale, scaled, cols):
    wide = feats.astype(F32)
    squares = split3(-scale * jnp.sum(wide * wide, axis=0, keepdims=True))
    parts = split3((2.0 * scale) * wide) if scaled else (feats,) * 3
    for k in range(3):
        dst[32 * k : 32 * (k + 1), cols] = parts[k]
    dst[96:128, cols] = tail_rows(squares, 3 if scaled else 0, 0 if scaled else 3)


def dot(a, b):
    return jnp.dot(a, b, preferred_element_type=F32)


def dot_nt(a, b):
    return lax.dot_general(a, b, (((1,), (1,)), ((), ())), preferred_element_type=F32)


def kernel(
    feats, outs, n_pts, n_cen, total_pts,
    p_ref, z_ref, out_ref,
    bpts, bown, arow, kta, ktb, tilea, tileb, fpart, zslots, zaug, mmacc, fwd,
    sbuf, dbuf, rsend, rrecv, dsend, drecv, outt,
    a_send, a_recv, d1_send, d1_recv, rs_send, rs_recv, ag_send, ag_recv,
    d2_send, d2_recv, ds_send, ds_recv, dg_send, dg_recv,
):
    scale = math.log2(math.e) * 2.0 / feats
    norm = float(np.float32(1.0) / np.sqrt(np.float32(total_pts)))
    d, c = lax.axis_index("dp"), lax.axis_index("centers")
    core, x_lo, z = c % 2, (c // 2) % 2, c // 4
    chip = c // 2
    y, x_hi = d // 2, d % 2
    kts, tiles = (kta, ktb), (tilea, tileb)
    half = outs // 2
    r_own = pl.multiple_of(half * core, half)
    r_other = pl.multiple_of(half * (1 - core), half)
    cpts = n_pts // CHUNKS
    share = cpts // 16
    dshare = n_cen // 8

    def at(dp, cen):
        return {"dp": dp, "centers": cen}

    partner = at(d, chip * 2 + 1 - core)
    x_next = at(d, z * 4 + (1 - x_lo) * 2 + core)

    def chip_peer(k):
        return (chip + k) % 16

    def group(k):
        return at(d, chip_peer(k) * 2 + core)

    def dp_peer(k):
        return (d + k) % 8

    def remote(src, dst, send, recv, dev):
        return pltpu.make_async_remote_copy(
            src_ref=src, dst_ref=dst, send_sem=send, recv_sem=recv, device_id=dev, device_id_type=MESH
        )

    barrier = pltpu.get_barrier_semaphore()
    for k in range(1, 16):
        pl.semaphore_signal(barrier, inc=1, device_id=group(k), device_id_type=MESH)
    pl.semaphore_signal(barrier, inc=1, device_id=partner, device_id_type=MESH)
    for k in range(1, 8):
        pl.semaphore_signal(barrier, inc=1, device_id=at(dp_peer(k), c), device_id_type=MESH)

    def prep_own(t, _):
        cols = pl.ds(pl.multiple_of(t * TILE, TILE), TILE)
        fill(bown, z_ref[0:feats, cols], scale, True, cols)
        arow[cols, :] = bown[:, cols].T
        return 0

    def prep_pts(t, _):
        cols = pl.ds(pl.multiple_of(t * 512, 512), 512)
        for e in range(2):
            fill(bpts.at[e], p_ref[:, pl.ds(pl.multiple_of(e * (n_pts // 2) + t * 512, 512), 512)], scale, False, cols)
        return 0

    with jax.named_scope("prep"):
        lax.fori_loop(0, n_cen // TILE, prep_own, 0)
        lax.fori_loop(0, n_pts // 1024, prep_pts, 0)

    dz = (y + 4 * ((x_hi + core) % 2)) % 8
    far = jnp.where((dz >= 3) & (dz <= 6), 1, 0)
    hcen = n_cen // 2

    def part(ref, h):
        return ref.at[:, h * hcen : (h + 1) * hcen]

    def a_z(h):
        dest = at(d, ((z + 8 - dz) % 8) * 4 + x_lo * 2 + core)
        return remote(part(z_ref, h), part(zslots.at[2 * far], h), a_send.at[0, h], a_recv.at[2 * far, h], dest)

    def a_local(h):
        return pltpu.make_async_copy(part(z_ref, h), part(zslots.at[2 * far], h), a_recv.at[2 * far, h])

    def a_x(slot, h):
        return remote(part(zslots.at[slot], h), part(zslots.at[slot + 1], h), a_send.at[1, h], a_recv.at[slot + 1, h], x_next)

    def a_core(slot, h):
        where = part(zslots.at[slot], h)
        return remote(where, where, a_send.at[2 + slot % 2, h], a_recv.at[slot, h], partner)

    def a_arrived(slot, h):
        where = part(zslots.at[slot], h)
        pltpu.make_async_copy(where, where, a_recv.at[slot, h]).wait()

        @pl.when(far == slot // 2)
        def _():
            a_core(slot, h).start()
            if slot % 2 == 0:
                a_x(slot, h).start()

    def nm_tiles(t, ref):
        cols = pl.ds(pl.multiple_of(t * WIDE, WIDE), WIDE)
        right = bpts[ref, :, cols]
        for b in range(n_cen // TILE):
            rows = pl.ds(b * TILE, TILE)
            kts[ref][rows, cols] = jnp.exp2(dot(arow[rows, :], right)).astype(BF16)

    def nm_sum(t, ref):
        cols = pl.ds(pl.multiple_of(t * WIDE, WIDE), WIDE)
        fpart[ref, :, cols] = dot(z_ref[feats : feats + outs, :], kts[ref][:, cols])

    def nm_step(t, first):
        if not first:
            nm_sum(t - 1, 1)
        nm_tiles(t, 0)
        nm_sum(t, 0)
        nm_tiles(t, 1)

    def nm(lo, hi):
        def step(t, _):
            nm_step(t, False)
            return 0

        lax.fori_loop(lo, hi, step, 0)

    piece = cpts // 2

    def d1(q):
        return remote(sbuf.at[q], dbuf.at[q], d1_send.at[q], d1_recv.at[q], partner)

    def d1_go(q):
        for e in range(2):
            sbuf[q, :, e * piece : (e + 1) * piece] = fpart[e, pl.ds(r_other, half), q * piece : (q + 1) * piece].astype(BF16)
        d1(q).start()

    def rs(q, k):
        lanes = pl.ds(pl.multiple_of(chip_peer(k) * share, share), share)
        return remote(rsend.at[q, :, lanes], rrecv.at[q, k], rs_send.at[q, k], rs_recv.at[q, k], group(k))

    own_rows = pl.ds(r_own, half)

    def rs_go(q):
        d1(q).wait_recv()
        for e in range(2):
            lanes = slice(e * piece, (e + 1) * piece)
            mine = fpart[e, own_rows, q * piece : (q + 1) * piece]
            rsend[q, :, lanes] = (mine + dbuf[q, :, lanes].astype(F32)).astype(BF16)
        for k in range(1, 16):
            rs(q, k).start()

    def own_share(q):
        return (chip // 8, own_rows, pl.ds(pl.multiple_of(q * piece + (chip % 8) * share, share), share))

    def ag(q, k):
        where = fwd.at[own_share(q)]
        return remote(where, where, ag_send.at[q, k], ag_recv.at[q, k], group(k))

    def ag_go(q):
        total = rsend[q, :, pl.ds(pl.multiple_of(chip * share, share), share)].astype(F32)
        for k in range(1, 16):
            rs(q, k).wait_recv()
            total = total + rrecv[q, k].astype(F32)
        fwd[own_share(q)] = total.astype(BF16)
        for k in range(1, 16):
            ag(q, k).start()

    def d2(q):
        where = fwd.at[:, own_rows, q * piece : (q + 1) * piece]
        return remote(where, where, d2_send.at[q], d2_recv.at[q], partner)

    def d2_go(q):
        for k in range(1, 16):
            ag(q, k).wait_recv()
        d2(q).start()

    blocks = n_cen // WIDE // 2

    def mm_prep(slot, h):
        def step(t, _):
            cols = pl.ds(pl.multiple_of(t * 512, 512), 512)
            fill(zaug, zslots[slot, 0:feats, cols], scale, False, cols)
            return 0

        lax.fori_loop(h * hcen // 512, (h + 1) * hcen // 512, step, 0)

    def mm_tiles(g, ref):
        start = (g % blocks) * (2 * WIDE) + ref * WIDE
        left = zaug[:, pl.ds(pl.multiple_of(start, WIDE), WIDE)].T
        for b in range(n_cen // TILE):
            cols = pl.ds(b * TILE, TILE)
            tiles[ref][:, cols] = jnp.exp2(dot(left, bown[:, cols])).astype(BF16)

    def mm_sum(slot, g, ref, first=False):
        start = (g % blocks) * (2 * WIDE) + ref * WIDE
        weights = zslots[slot, feats : feats + outs, pl.ds(pl.multiple_of(start, WIDE), WIDE)]
        for b in range(n_cen // TILE):
            cols = pl.ds(b * TILE, TILE)
            one = dot(weights, tiles[ref][:, cols])
            mmacc[:, cols] = one if first else mmacc[:, cols] + one

    def mm(body, last):
        slot, h = body
        mm_prep(slot, h)
        if last is not None:
            mm_sum(*last, 1)
        mm_tiles(h, 0)
        mm_sum(slot, h, 0, first=last is None)
        mm_tiles(h, 1)

    with jax.named_scope("nm_a"):
        nm_step(0, True)
    with jax.named_scope("barrier"):
        pl.semaphore_wait(barrier, 23)

    @pl.when(dz != 0)
    def _():
        for h in range(2):
            a_z(h).start()

    @pl.when(dz == 0)
    def _():
        for h in range(2):
            a_local(h).start()

    steps = n_pts // WIDE // 2
    with jax.named_scope("nm_b"):
        nm(1, steps // 2 + 1)
    with jax.named_scope("d1_0"):
        d1_go(0)
    with jax.named_scope("nm_c"):
        nm(steps // 2 + 1, steps)
        nm_sum(steps - 1, 1)
    with jax.named_scope("d1_1"):
        d1_go(1)
    with jax.named_scope("rs_0"):
        rs_go(0)
    order = [(0, 0), (0, 1), (1, 0), (1, 1), (2, 0), (3, 0), (2, 1), (3, 1)]
    after = {0: lambda: rs_go(1), 1: lambda: ag_go(0), 3: lambda: ag_go(1), 5: lambda: d2_go(0), 6: lambda: d2_go(1)}
    early = {2: [(2, 0)], 5: [(2, 1)]}
    done = set()
    for n, body in enumerate(order):
        with jax.named_scope(f"a_{n}"):
            for what in early.get(n, []) + [body]:
                if what not in done:
                    a_arrived(*what)
                    done.add(what)
        with jax.named_scope(f"mm_{n}"):
            mm(body, order[n - 1] if n else None)
        if n in after:
            with jax.named_scope(f"after_{n}"):
                after[n]()
    with jax.named_scope("mm_end"):
        mm_sum(*order[-1], 1)
    with jax.named_scope("d2_wait"):
        d2(0).wait_recv()
        d2(1).wait_recv()

    def back(k):
        rows = pl.ds(pl.multiple_of(dp_peer(k) * dshare, dshare), dshare)
        total = dot_nt(fwd[0], kta[rows, :]) + dot_nt(fwd[1], ktb[rows, :])
        return total * norm + mmacc[:, rows]

    def ds_copy(k):
        return remote(dsend.at[k], drecv.at[k], ds_send.at[k], ds_recv.at[k], at(dp_peer(k), c))

    def back_step(k, _):
        dsend[k] = back(k)
        ds_copy(k).start()
        return 0

    with jax.named_scope("back"):
        lax.fori_loop(1, 8, back_step, 0)
    with jax.named_scope("back0_dswait"):
        total = back(0)
        for k in range(1, 8):
            ds_copy(k).wait_recv()
            total = total + drecv[k]
    mine = pl.ds(pl.multiple_of(d * dshare, dshare), dshare)
    outt[:, mine] = total

    def dg(k):
        return remote(outt.at[:, mine], outt.at[:, mine], dg_send.at[k], dg_recv.at[k], at(dp_peer(k), c))

    for k in range(1, 8):
        dg(k).start()

    for h in range(2):

        @pl.when(dz != 0)
        def _():
            a_z(h).wait_send()

        a_x(0, h).wait_send()
        a_core(0, h).wait_send()
        a_core(1, h).wait_send()
    for q in range(CHUNKS):
        d1(q).wait_send()
        d2(q).wait_send()
        for k in range(1, 16):
            rs(q, k).wait_send()
            ag(q, k).wait_send()
    for k in range(1, 8):
        ds_copy(k).wait_send()
    with jax.named_scope("dg_wait_out"):
        for k in range(1, 8):
            dg(k).wait_recv()
        out_ref[...] = outt[...].T
    for k in range(1, 8):
        dg(k).wait_send()


def solution(mesh):
    def on_device(points, centers, coef):
        n_pts, feats = points.shape
        n_cen, outs = coef.shape
        cpts = n_pts // CHUNKS
        dma = pltpu.SemaphoreType.DMA
        stacked = jnp.concatenate((centers, coef), axis=1).T

        def body(*refs):
            kernel(feats, outs, n_pts, n_cen, n_pts * 8, *refs)

        return pl.pallas_call(
            body,
            out_shape=jax.ShapeDtypeStruct((n_cen, outs), F32),
            in_specs=[pl.BlockSpec(memory_space=pltpu.VMEM)] * 2,
            out_specs=pl.BlockSpec(memory_space=pltpu.VMEM),
            scratch_shapes=[
                pltpu.VMEM((2, ROWS, n_pts // 2), BF16),
                pltpu.VMEM((ROWS, n_cen), BF16),
                pltpu.VMEM((n_cen, ROWS), BF16),
                pltpu.VMEM((n_cen, n_pts // 2), BF16),
                pltpu.VMEM((n_cen, n_pts // 2), BF16),
                pltpu.VMEM((WIDE, n_cen), BF16),
                pltpu.VMEM((WIDE, n_cen), BF16),
                pltpu.VMEM((2, outs, n_pts // 2), F32),
                pltpu.VMEM((4, feats + outs, n_cen), BF16),
                pltpu.VMEM((ROWS, n_cen), BF16),
                pltpu.VMEM((outs, n_cen), F32),
                pltpu.VMEM((2, outs, n_pts // 2), BF16),
                pltpu.VMEM((CHUNKS, outs // 2, cpts), BF16),
                pltpu.VMEM((CHUNKS, outs // 2, cpts), BF16),
                pltpu.VMEM((CHUNKS, outs // 2, cpts), BF16),
                pltpu.VMEM((CHUNKS, 16, outs // 2, cpts // 16), BF16),
                pltpu.VMEM((8, outs, n_cen // 8), F32),
                pltpu.VMEM((8, outs, n_cen // 8), F32),
                pltpu.VMEM((outs, n_cen), F32),
                dma((4, 2)), dma((4, 2)),
                dma((CHUNKS,)), dma((CHUNKS,)),
                dma((CHUNKS, 16)), dma((CHUNKS, 16)),
                dma((CHUNKS, 16)), dma((CHUNKS, 16)),
                dma((CHUNKS,)), dma((CHUNKS,)),
                dma((8,)), dma((8,)),
                dma((8,)), dma((8,)),
            ],
            compiler_params=pltpu.CompilerParams(
                collective_id=0, has_side_effects=True, vmem_limit_bytes=60 * 1024 * 1024
            ),
        )(points.T, stacked)

    in_specs = (P("dp", None), P("centers", None), P("centers", None))
    return jax.shard_map(
        on_device, mesh=mesh, in_specs=in_specs, out_specs=P("centers", None), check_vma=False
    )
```

time: 75.9 us -> 76.7 us (1.011)
  no operation moved by 1% of the time
where the time goes in v3:
time: 76.7 us; the launch traced here: 76.5 us
  Pallas kernels  72.4 us (94%)
  local copies, waits for them, and re-layouts  2.34 us (3%)
  other arithmetic  1.75 us (2%)
    pallas_call x1, Pallas kernels, on_device(): pl.pallas_call(body, out_shape=jax.ShapeDtypeStruct((n_cen, outs), F32),...  72.4 us
    pallas_call x1, local copies, waits for them, and re-layouts, on_device(): pl.pallas_call(body, out_shape=jax.ShapeDtypeStruct((n_cen, outs), F32),...  2.34 us
    transpose x1, other arithmetic, on_device(): stacked = jnp.concatenate((centers, coef), axis=1).T  1.75 us

profile of v3, /device:TPU:1, one launch (start us, length us, event | category | flops | bytes accessed | tf_op | source)
XLA Modules:
  0.0 76.5 jit_solution(15281095566589644711)
XLA Ops:
  0.0 1.8 %maximum_bitcast_fusion.refs_1_ = bf16[96,2048]{1,0:T(8,128)(2,1)} fusion(bf16[2048,64]{0,1:T(8,128)(2,1)} %param.5, bf16[2048,32]{0,1:T(8,128)(2,1)} %param.4), kind=kLoop, calls=%fused_computation | loop fusion | flops 786432 | bytes 786432 | tf_op jit(solution)/shard_map/transpose | solution.py:365
  1.8 72.4 %shard_map.37 = f32[2048,64]{1,0:T(8,128)} custom-call(bf16[32,4096]{1,0:T(8,128)(2,1)} %bitcast.3, bf16[96,2048]{1,0:T(8,128)(2,1)} %maximum_bitcast_fusion.refs_1_), custom_call_target="tpu_custom_call" | custom-call | tf_op jit(solution)/shard_map/pallas_call | solution.py:370
  74.2 2.3 %copy.4 = f32[2048,64]{0,1:T(8,128)} copy(f32[2048,64]{1,0:T(8,128)} %shard_map.37) | data formatting | bytes 1048576 | tf_op jit(solution)/shard_map/pallas_call | solution.py:370

commit v4 on v3

--- a/solution.py
+++ b/solution.py
@@ -52,9 +52,10 @@
 def kernel(
     feats, outs, n_pts, n_cen, total_pts,
     p_ref, z_ref, out_ref,
-    bpts, bown, arow, kta, ktb, tilea, tileb, fpart, zslots, zaug, mmacc, fwd,
+    bpts, bown, arow, kta, ktb, tilea, tileb, fpart, zbuf, zaug, mmacc, fwd,
     sbuf, dbuf, rsend, rrecv, dsend, drecv, outt,
-    a_send, a_recv, d1_send, d1_recv, rs_send, rs_recv, ag_send, ag_recv,
+    z_send, z_recv, x_send, x_recv, c1_send, c1_recv, c3_send, c3_recv,
+    d1_send, d1_recv, rs_send, rs_recv, ag_send, ag_recv,
     d2_send, d2_recv, ds_send, ds_recv, dg_send, dg_recv,
 ):
     scale = math.log2(math.e) * 2.0 / feats
@@ -114,36 +115,45 @@
         lax.fori_loop(0, n_cen // TILE, prep_own, 0)
         lax.fori_loop(0, n_pts // 1024, prep_pts, 0)
 
-    dz = (y + 4 * ((x_hi + core) % 2)) % 8
-    far = jnp.where((dz >= 3) & (dz <= 6), 1, 0)
-    hcen = n_cen // 2
-
-    def part(ref, h):
-        return ref.at[:, h * hcen : (h + 1) * hcen]
-
-    def a_z(h):
-        dest = at(d, ((z + 8 - dz) % 8) * 4 + x_lo * 2 + core)
-        return remote(part(z_ref, h), part(zslots.at[2 * far], h), a_send.at[0, h], a_recv.at[2 * far, h], dest)
-
-    def a_local(h):
-        return pltpu.make_async_copy(part(z_ref, h), part(zslots.at[2 * far], h), a_recv.at[2 * far, h])
-
-    def a_x(slot, h):
-        return remote(part(zslots.at[slot], h), part(zslots.at[slot + 1], h), a_send.at[1, h], a_recv.at[slot + 1, h], x_next)
-
-    def a_core(slot, h):
-        where = part(zslots.at[slot], h)
-        return remote(where, where, a_send.at[2 + slot % 2, h], a_recv.at[slot, h], partner)
-
-    def a_arrived(slot, h):
-        where = part(zslots.at[slot], h)
-        pltpu.make_async_copy(where, where, a_recv.at[slot, h]).wait()
-
-        @pl.when(far == slot // 2)
-        def _():
-            a_core(slot, h).start()
-            if slot % 2 == 0:
-                a_x(slot, h).start()
+    part = n_cen // 8
+    own_part = (slice(None), pl.ds(pl.multiple_of(d * part, part), part))
+
+    def place(slab, pos):
+        return zbuf.at[slab, :, pos * part : (pos + 1) * part]
+
+    def a_z(slab):
+        up = slab % 2
+        dest = at(d, ((z + (1 if up else 7)) % 8) * 4 + x_lo * 2 + core)
+        src = z_ref.at[own_part] if slab <= 2 else place(slab - 2, 0)
+        return remote(src, place(slab, 0), z_send.at[slab], z_recv.at[slab], dest)
+
+    def a_mine(slab):
+        return z_ref.at[own_part] if slab == 0 else place(slab, 0)
+
+    def a_x(slab):
+        return remote(a_mine(slab), place(slab, 2), x_send.at[slab], x_recv.at[slab], x_next)
+
+    def a_core(slab):
+        return remote(a_mine(slab), place(slab, 1), c1_send.at[slab], c1_recv.at[slab], partner)
+
+    def a_cross(slab):
+        return remote(place(slab, 2), place(slab, 3), c3_send.at[slab], c3_recv.at[slab], partner)
+
+    def z_came(slab):
+        a_z(slab).wait_recv()
+        if slab + 2 <= 7:
+            a_z(slab + 2).start()
+        a_x(slab).start()
+        a_core(slab).start()
+
+    def x_came(slab):
+        a_x(slab).wait_recv()
+        a_cross(slab).start()
+
+    def slab_ready(slab):
+        where = zbuf.at[slab, :, 0:part]
+        pltpu.make_async_copy(where, where, c1_recv.at[slab]).wait()
+        pltpu.make_async_copy(where, where, c3_recv.at[slab]).wait()
 
     def nm_tiles(t, ref):
         cols = pl.ds(pl.multiple_of(t * WIDE, WIDE), WIDE)
@@ -162,13 +172,6 @@
         nm_tiles(t, 0)
         nm_sum(t, 0)
         nm_tiles(t, 1)
-
-    def nm(lo, hi):
-        def step(t, _):
-            nm_step(t, False)
-            return 0
-
-        lax.fori_loop(lo, hi, step, 0)
 
     piece = cpts // 2
 
@@ -220,84 +223,96 @@
             ag(q, k).wait_recv()
         d2(q).start()
 
-    blocks = n_cen // WIDE // 2
-
-    def mm_prep(slot, h):
-        def step(t, _):
-            cols = pl.ds(pl.multiple_of(t * 512, 512), 512)
-            fill(zaug, zslots[slot, 0:feats, cols], scale, False, cols)
-            return 0
-
-        lax.fori_loop(h * hcen // 512, (h + 1) * hcen // 512, step, 0)
-
-    def mm_tiles(g, ref):
-        start = (g % blocks) * (2 * WIDE) + ref * WIDE
-        left = zaug[:, pl.ds(pl.multiple_of(start, WIDE), WIDE)].T
+    def mm_prep(slab):
+        for h in range(2):
+            cols = slice(h * WIDE, (h + 1) * WIDE)
+            fill(zaug, zbuf[slab, 0:feats, cols], scale, False, cols)
+
+    def mm_tiles(ref):
+        left = zaug[:, ref * WIDE : (ref + 1) * WIDE].T
         for b in range(n_cen // TILE):
             cols = pl.ds(b * TILE, TILE)
             tiles[ref][:, cols] = jnp.exp2(dot(left, bown[:, cols])).astype(BF16)
 
-    def mm_sum(slot, g, ref, first=False):
-        start = (g % blocks) * (2 * WIDE) + ref * WIDE
-        weights = zslots[slot, feats : feats + outs, pl.ds(pl.multiple_of(start, WIDE), WIDE)]
+    def mm_sum(slab, ref, first=False):
+        weights = zbuf[slab, feats : feats + outs, ref * WIDE : (ref + 1) * WIDE]
         for b in range(n_cen // TILE):
             cols = pl.ds(b * TILE, TILE)
             one = dot(weights, tiles[ref][:, cols])
             mmacc[:, cols] = one if first else mmacc[:, cols] + one
 
-    def mm(body, last):
-        slot, h = body
-        mm_prep(slot, h)
-        if last is not None:
-            mm_sum(*last, 1)
-        mm_tiles(h, 0)
-        mm_sum(slot, h, 0, first=last is None)
-        mm_tiles(h, 1)
-
+    def mm(slab, first):
+        slab_ready(slab)
+        mm_prep(slab)
+        if not first:
+            mm_sum(slab - 1, 1)
+        mm_tiles(0)
+        mm_sum(slab, 0, first)
+        mm_tiles(1)
+
+    def actions(n, table):
+        for step, todo in table.items():
+
+            @pl.when(n == step)
+            def _():
+                for f, q in todo:
+                    f(q)
+
+    steps = n_pts // WIDE // 2
     with jax.named_scope("nm_a"):
         nm_step(0, True)
     with jax.named_scope("barrier"):
         pl.semaphore_wait(barrier, 23)
-
-    @pl.when(dz != 0)
-    def _():
-        for h in range(2):
-            a_z(h).start()
-
-    @pl.when(dz == 0)
-    def _():
-        for h in range(2):
-            a_local(h).start()
-
-    steps = n_pts // WIDE // 2
-    with jax.named_scope("nm_b"):
-        nm(1, steps // 2 + 1)
-    with jax.named_scope("d1_0"):
-        d1_go(0)
-    with jax.named_scope("nm_c"):
-        nm(steps // 2 + 1, steps)
+    a_z(1).start()
+    a_z(2).start()
+    a_x(0).start()
+    a_core(0).start()
+    zbuf[0, :, 0:part] = z_ref[own_part]
+
+    def nm_body(n, _):
+        with jax.named_scope("nm_body"):
+            nm_step(n, False)
+        with jax.named_scope("nm_act"):
+            actions(n, {2: [(d1_go, 0), (z_came, 1), (z_came, 2), (x_came, 0)]})
+        return 0
+
+    lax.fori_loop(1, steps, nm_body, 0)
+    with jax.named_scope("nm_end"):
         nm_sum(steps - 1, 1)
-    with jax.named_scope("d1_1"):
+    with jax.named_scope("nm_end_act"):
         d1_go(1)
-    with jax.named_scope("rs_0"):
         rs_go(0)
-    order = [(0, 0), (0, 1), (1, 0), (1, 1), (2, 0), (3, 0), (2, 1), (3, 1)]
-    after = {0: lambda: rs_go(1), 1: lambda: ag_go(0), 3: lambda: ag_go(1), 5: lambda: d2_go(0), 6: lambda: d2_go(1)}
-    early = {2: [(2, 0)], 5: [(2, 1)]}
-    done = set()
-    for n, body in enumerate(order):
-        with jax.named_scope(f"a_{n}"):
-            for what in early.get(n, []) + [body]:
-                if what not in done:
-                    a_arrived(*what)
-                    done.add(what)
-        with jax.named_scope(f"mm_{n}"):
-            mm(body, order[n - 1] if n else None)
-        if n in after:
-            with jax.named_scope(f"after_{n}"):
-                after[n]()
+        z_came(3)
+        z_came(4)
+
+    with jax.named_scope("mm_0"):
+        mm(0, True)
+    with jax.named_scope("mm_0_act"):
+        rs_go(1)
+        z_came(5)
+        z_came(6)
+        x_came(1)
+        x_came(2)
+
+    table = {
+        1: [(z_came, 7), (x_came, 3)],
+        2: [(ag_go, 0), (x_came, 4)],
+        3: [(x_came, 5)],
+        4: [(ag_go, 1), (x_came, 6)],
+        5: [(x_came, 7), (d2_go, 0)],
+        6: [(d2_go, 1)],
+    }
+
+    def mm_body(n, _):
+        with jax.named_scope("mm_body"):
+            mm(n, False)
+        with jax.named_scope("mm_act"):
+            actions(n, table)
+        return 0
+
+    lax.fori_loop(1, 8, mm_body, 0)
     with jax.named_scope("mm_end"):
-        mm_sum(*order[-1], 1)
+        mm_sum(7, 1)
     with jax.named_scope("d2_wait"):
         d2(0).wait_recv()
         d2(1).wait_recv()
@@ -331,15 +346,12 @@
     for k in range(1, 8):
         dg(k).start()
 
-    for h in range(2):
-
-        @pl.when(dz != 0)
-        def _():
-            a_z(h).wait_send()
-
-        a_x(0, h).wait_send()
-        a_core(0, h).wait_send()
-        a_core(1, h).wait_send()
+    for slab in range(8):
+        if slab:
+            a_z(slab).wait_send()
+        a_x(slab).wait_send()
+        a_core(slab).wait_send()
+        a_cross(slab).wait_send()
     for q in range(CHUNKS):
         d1(q).wait_send()
         d2(q).wait_send()
@@ -381,8 +393,8 @@
                 pltpu.VMEM((WIDE, n_cen), BF16),
                 pltpu.VMEM((WIDE, n_cen), BF16),
                 pltpu.VMEM((2, outs, n_pts // 2), F32),
-                pltpu.VMEM((4, feats + outs, n_cen), BF16),
-                pltpu.VMEM((ROWS, n_cen), BF16),
+                pltpu.VMEM((8, feats + outs, n_cen // 2), BF16),
+                pltpu.VMEM((ROWS, n_cen // 2), BF16),
                 pltpu.VMEM((outs, n_cen), F32),
                 pltpu.VMEM((2, outs, n_pts // 2), BF16),
                 pltpu.VMEM((CHUNKS, outs // 2, cpts), BF16),
@@ -392,7 +404,7 @@
                 pltpu.VMEM((8, outs, n_cen // 8), F32),
                 pltpu.VMEM((8, outs, n_cen // 8), F32),
                 pltpu.VMEM((outs, n_cen), F32),
-                dma((4, 2)), dma((4, 2)),
+                *[dma((8,))] * 8,
                 dma((CHUNKS,)), dma((CHUNKS,)),
                 dma((CHUNKS, 16)), dma((CHUNKS, 16)),
                 dma((CHUNKS, 16)), dma((CHUNKS, 16)),

time: 76.7 us -> 68.5 us (0.89)
  Pallas kernels: 72.4 us -> 64.2 us
    pallas_call x1, Pallas kernels: 72.4 us -> 64.2 us  [on_device(): pl.pallas_call(body, out_shape=jax.ShapeDtypeStruct((n_cen, outs), F32),...]
where the time goes in v4:
time: 68.5 us; the launch traced here: 68.3 us
  Pallas kernels  64.2 us (94%)
  local copies, waits for them, and re-layouts  2.34 us (3%)
  other arithmetic  1.75 us (3%)
    pallas_call x1, Pallas kernels, on_device(): pl.pallas_call(body, out_shape=jax.ShapeDtypeStruct((n_cen, outs), F32),...  64.2 us
    pallas_call x1, local copies, waits for them, and re-layouts, on_device(): pl.pallas_call(body, out_shape=jax.ShapeDtypeStruct((n_cen, outs), F32),...  2.34 us
    transpose x1, other arithmetic, on_device(): stacked = jnp.concatenate((centers, coef), axis=1).T  1.75 us

profile of v4, /device:TPU:1, one launch (start us, length us, event | category | flops | bytes accessed | tf_op | source)
XLA Modules:
  0.0 68.3 jit_solution(11767572500191104107)
XLA Ops:
  0.0 1.8 %maximum_bitcast_fusion.refs_1_ = bf16[96,2048]{1,0:T(8,128)(2,1)} fusion(bf16[2048,64]{0,1:T(8,128)(2,1)} %param.5, bf16[2048,32]{0,1:T(8,128)(2,1)} %param.4), kind=kLoop, calls=%fused_computation | loop fusion | flops 786432 | bytes 786432 | tf_op jit(solution)/shard_map/transpose | solution.py:377
  1.8 64.2 %shard_map.37 = f32[2048,64]{1,0:T(8,128)} custom-call(bf16[32,4096]{1,0:T(8,128)(2,1)} %bitcast.3, bf16[96,2048]{1,0:T(8,128)(2,1)} %maximum_bitcast_fusion.refs_1_), custom_call_target="tpu_custom_call" | custom-call | tf_op jit(solution)/shard_map/pallas_call | solution.py:382
  66.0 2.3 %copy.4 = f32[2048,64]{0,1:T(8,128)} copy(f32[2048,64]{1,0:T(8,128)} %shard_map.37) | data formatting | bytes 1048576 | tf_op jit(solution)/shard_map/pallas_call | solution.py:382

commit v5 on v4

--- a/solution.py
+++ b/solution.py
@@ -51,10 +51,10 @@
 
 def kernel(
     feats, outs, n_pts, n_cen, total_pts,
-    p_ref, z_ref, out_ref,
+    p_ref, c_ref, w_ref, out_ref,
     bpts, bown, arow, kta, ktb, tilea, tileb, fpart, zbuf, zaug, mmacc, fwd,
     sbuf, dbuf, rsend, rrecv, dsend, drecv, outt,
-    z_send, z_recv, x_send, x_recv, c1_send, c1_recv, c3_send, c3_recv,
+    z_send, z_recv, x_send, x_recv, c1_send, c1_recv, c3_send, c3_recv, own_sem,
     d1_send, d1_recv, rs_send, rs_recv, ag_send, ag_recv,
     d2_send, d2_recv, ds_send, ds_recv, dg_send, dg_recv,
 ):
@@ -101,7 +101,7 @@
 
     def prep_own(t, _):
         cols = pl.ds(pl.multiple_of(t * TILE, TILE), TILE)
-        fill(bown, z_ref[0:feats, cols], scale, True, cols)
+        fill(bown, c_ref[:, cols], scale, True, cols)
         arow[cols, :] = bown[:, cols].T
         return 0
 
@@ -116,25 +116,25 @@
         lax.fori_loop(0, n_pts // 1024, prep_pts, 0)
 
     part = n_cen // 8
-    own_part = (slice(None), pl.ds(pl.multiple_of(d * part, part), part))
+    own_part = pl.ds(pl.multiple_of(d * part, part), part)
 
     def place(slab, pos):
-        return zbuf.at[slab, :, pos * part : (pos + 1) * part]
+        if slab in (0, 7):
+            body, at_pos = slab, pos
+        else:
+            first = (slab + 1) // 2 * 2 - 1
+            body, at_pos = first + pos // 2, 2 * (slab - first) + pos % 2
+        return zbuf.at[body, :, at_pos * part : (at_pos + 1) * part]
 
     def a_z(slab):
-        up = slab % 2
-        dest = at(d, ((z + (1 if up else 7)) % 8) * 4 + x_lo * 2 + core)
-        src = z_ref.at[own_part] if slab <= 2 else place(slab - 2, 0)
-        return remote(src, place(slab, 0), z_send.at[slab], z_recv.at[slab], dest)
-
-    def a_mine(slab):
-        return z_ref.at[own_part] if slab == 0 else place(slab, 0)
+        dest = at(d, ((z + (1 if slab % 2 else 7)) % 8) * 4 + x_lo * 2 + core)
+        return remote(place(max(slab - 2, 0), 0), place(slab, 0), z_send.at[slab], z_recv.at[slab], dest)
 
     def a_x(slab):
-        return remote(a_mine(slab), place(slab, 2), x_send.at[slab], x_recv.at[slab], x_next)
+        return remote(place(slab, 0), place(slab, 2), x_send.at[slab], x_recv.at[slab], x_next)
 
     def a_core(slab):
-        return remote(a_mine(slab), place(slab, 1), c1_send.at[slab], c1_recv.at[slab], partner)
+        return remote(place(slab, 0), place(slab, 1), c1_send.at[slab], c1_recv.at[slab], partner)
 
     def a_cross(slab):
         return remote(place(slab, 2), place(slab, 3), c3_send.at[slab], c3_recv.at[slab], partner)
@@ -143,17 +143,26 @@
         a_z(slab).wait_recv()
         if slab + 2 <= 7:
             a_z(slab + 2).start()
+        a_core(slab).start()
         a_x(slab).start()
-        a_core(slab).start()
 
     def x_came(slab):
         a_x(slab).wait_recv()
         a_cross(slab).start()
 
-    def slab_ready(slab):
-        where = zbuf.at[slab, :, 0:part]
-        pltpu.make_async_copy(where, where, c1_recv.at[slab]).wait()
-        pltpu.make_async_copy(where, where, c3_recv.at[slab]).wait()
+    def arrived(body, h):
+        if body in (0, 7):
+            (a_cross if h else a_core)(body).wait_recv()
+        else:
+            slab = (body - 1) // 2 * 2 + 1 + h
+            (a_core if body % 2 else a_cross)(slab).wait_recv()
+
+    a_own = [
+        pltpu.make_async_copy(src.at[:, own_part], zbuf.at[0, lo : lo + src.shape[0], 0:part], own_sem.at[n])
+        for n, (src, lo) in enumerate(((c_ref, 0), (w_ref, feats)))
+    ]
+    for copy in a_own:
+        copy.start()
 
     def nm_tiles(t, ref):
         cols = pl.ds(pl.multiple_of(t * WIDE, WIDE), WIDE)
@@ -164,7 +173,7 @@
 
     def nm_sum(t, ref):
         cols = pl.ds(pl.multiple_of(t * WIDE, WIDE), WIDE)
-        fpart[ref, :, cols] = dot(z_ref[feats : feats + outs, :], kts[ref][:, cols])
+        fpart[ref, :, cols] = dot(w_ref[...], kts[ref][:, cols])
 
     def nm_step(t, first):
         if not first:
@@ -223,32 +232,27 @@
             ag(q, k).wait_recv()
         d2(q).start()
 
-    def mm_prep(slab):
-        for h in range(2):
-            cols = slice(h * WIDE, (h + 1) * WIDE)
-            fill(zaug, zbuf[slab, 0:feats, cols], scale, False, cols)
-
-    def mm_tiles(ref):
-        left = zaug[:, ref * WIDE : (ref + 1) * WIDE].T
+    def mm_tiles(body, ref):
+        cols = slice(ref * WIDE, (ref + 1) * WIDE)
+        fill(zaug, zbuf[body, 0:feats, cols], scale, False, cols)
+        left = zaug[:, cols].T
         for b in range(n_cen // TILE):
             cols = pl.ds(b * TILE, TILE)
             tiles[ref][:, cols] = jnp.exp2(dot(left, bown[:, cols])).astype(BF16)
 
-    def mm_sum(slab, ref, first=False):
-        weights = zbuf[slab, feats : feats + outs, ref * WIDE : (ref + 1) * WIDE]
+    def mm_sum(body, ref, first=False):
+        weights = zbuf[body, feats : feats + outs, ref * WIDE : (ref + 1) * WIDE]
         for b in range(n_cen // TILE):
             cols = pl.ds(b * TILE, TILE)
             one = dot(weights, tiles[ref][:, cols])
             mmacc[:, cols] = one if first else mmacc[:, cols] + one
 
-    def mm(slab, first):
-        slab_ready(slab)
-        mm_prep(slab)
+    def mm(body, first):
         if not first:
-            mm_sum(slab - 1, 1)
-        mm_tiles(0)
-        mm_sum(slab, 0, first)
-        mm_tiles(1)
+            mm_sum(body - 1, 1)
+        mm_tiles(body, 0)
+        mm_sum(body, 0, first)
+        mm_tiles(body, 1)
 
     def actions(n, table):
         for step, todo in table.items():
@@ -263,11 +267,12 @@
         nm_step(0, True)
     with jax.named_scope("barrier"):
         pl.semaphore_wait(barrier, 23)
+    for copy in a_own:
+        copy.wait()
     a_z(1).start()
     a_z(2).start()
     a_x(0).start()
     a_core(0).start()
-    zbuf[0, :, 0:part] = z_ref[own_part]
 
     def nm_body(n, _):
         with jax.named_scope("nm_body"):
@@ -282,32 +287,42 @@
     with jax.named_scope("nm_end_act"):
         d1_go(1)
         rs_go(0)
-        z_came(3)
-        z_came(4)
+        arrived(0, 0)
+        arrived(0, 1)
 
     with jax.named_scope("mm_0"):
         mm(0, True)
     with jax.named_scope("mm_0_act"):
         rs_go(1)
-        z_came(5)
-        z_came(6)
+        z_came(3)
+        z_came(4)
         x_came(1)
         x_came(2)
+        arrived(1, 0)
+        arrived(1, 1)
 
     table = {
-        1: [(z_came, 7), (x_came, 3)],
-        2: [(ag_go, 0), (x_came, 4)],
-        3: [(x_came, 5)],
-        4: [(ag_go, 1), (x_came, 6)],
-        5: [(x_came, 7), (d2_go, 0)],
-        6: [(d2_go, 1)],
+        1: [],
+        2: [(z_came, 5), (z_came, 6), (x_came, 3), (x_came, 4), (ag_go, 0)],
+        3: [],
+        4: [(z_came, 7), (x_came, 5), (x_came, 6), (ag_go, 1)],
+        5: [(d2_go, 0)],
+        6: [(x_came, 7), (d2_go, 1)],
     }
 
     def mm_body(n, _):
         with jax.named_scope("mm_body"):
             mm(n, False)
         with jax.named_scope("mm_act"):
-            actions(n, table)
+            for step, todo in table.items():
+
+                @pl.when(n == step)
+                def _():
+                    for f, q in todo:
+                        f(q)
+                    arrived(step + 1, 0)
+                    arrived(step + 1, 1)
+
         return 0
 
     lax.fori_loop(1, 8, mm_body, 0)
@@ -363,7 +378,7 @@
     with jax.named_scope("dg_wait_out"):
         for k in range(1, 8):
             dg(k).wait_recv()
-        out_ref[...] = outt[...].T
+        out_ref[...] = outt[...]
     for k in range(1, 8):
         dg(k).wait_send()
 
@@ -374,15 +389,14 @@
         n_cen, outs = coef.shape
         cpts = n_pts // CHUNKS
         dma = pltpu.SemaphoreType.DMA
-        stacked = jnp.concatenate((centers, coef), axis=1).T
 
         def body(*refs):
             kernel(feats, outs, n_pts, n_cen, n_pts * 8, *refs)
 
         return pl.pallas_call(
             body,
-            out_shape=jax.ShapeDtypeStruct((n_cen, outs), F32),
-            in_specs=[pl.BlockSpec(memory_space=pltpu.VMEM)] * 2,
+            out_shape=jax.ShapeDtypeStruct((outs, n_cen), F32),
+            in_specs=[pl.BlockSpec(memory_space=pltpu.VMEM)] * 3,
             out_specs=pl.BlockSpec(memory_space=pltpu.VMEM),
             scratch_shapes=[
                 pltpu.VMEM((2, ROWS, n_pts // 2), BF16),
@@ -404,7 +418,7 @@
                 pltpu.VMEM((8, outs, n_cen // 8), F32),
                 pltpu.VMEM((8, outs, n_cen // 8), F32),
                 pltpu.VMEM((outs, n_cen), F32),
-                *[dma((8,))] * 8,
+                *[dma((8,))] * 8, dma((2,)),
                 dma((CHUNKS,)), dma((CHUNKS,)),
                 dma((CHUNKS, 16)), dma((CHUNKS, 16)),
                 dma((CHUNKS, 16)), dma((CHUNKS, 16)),
@@ -415,7 +429,7 @@
             compiler_params=pltpu.CompilerParams(
                 collective_id=0, has_side_effects=True, vmem_limit_bytes=60 * 1024 * 1024
             ),
-        )(points.T, stacked)
+        )(points.T, centers.T, coef.T).T
 
     in_specs = (P("dp", None), P("centers", None), P("centers", None))
     return jax.shard_map(

time: 68.5 us -> 63.5 us (0.927)
  Pallas kernels: 64.2 us -> 61.5 us
  other arithmetic: 1.75 us -> 0 us
    pallas_call x1, Pallas kernels: 64.2 us -> 61.5 us  [on_device(): pl.pallas_call(body, out_shape=jax.ShapeDtypeStruct((outs, n_cen), F32),...]
    pallas_call x1 -> x0, local copies, waits for them, and re-layouts: 2.34 us -> none  [on_device(): pl.pallas_call(body, out_shape=jax.ShapeDtypeStruct((n_cen, outs), F32),...]
    unnamed x0 -> x1, local copies, waits for them, and re-layouts: none -> 1.87 us
    transpose x1 -> x0, other arithmetic: 1.75 us -> none  [on_device(): stacked = jnp.concatenate((centers, coef), axis=1).T]
where the time goes in v5:
time: 63.5 us; the launch traced here: 63.4 us
  Pallas kernels  61.5 us (97%)
  local copies, waits for them, and re-layouts  1.87 us (3%)
    pallas_call x1, Pallas kernels, on_device(): pl.pallas_call(body, out_shape=jax.ShapeDtypeStruct((outs, n_cen), F32),...  61.5 us
    unnamed x1, local copies, waits for them, and re-layouts  1.87 us

profile of v5, /device:TPU:1, one launch (start us, length us, event | category | flops | bytes accessed | tf_op | source)
XLA Modules:
  0.0 63.4 jit_solution(11130926314498836574)
XLA Ops:
  0.0 61.5 %shard_map.37 = f32[64,2048]{1,0:T(8,128)} custom-call(bf16[32,4096]{1,0:T(8,128)(2,1)} %bitcast.5, bf16[32,2048]{1,0:T(8,128)(2,1)} %bitcast.7, bf16[64,2048]{1,0:T(8,128)(2,1)} %bitcast.6), custom_call_target="tpu_custom_call" | custom-call | tf_op jit(solution)/shard_map/pallas_call | solution.py:396
  61.5 1.9 %copy.5 = f32[2048,64]{0,1:T(8,128)} copy(f32[2048,64]{0,1:T(8,128)} %bitcast.4) | data formatting | bytes 1048576

commit v6 on v5

--- a/solution.py
+++ b/solution.py
@@ -164,23 +164,24 @@
     for copy in a_own:
         copy.start()
 
-    def nm_tiles(t, ref):
-        cols = pl.ds(pl.multiple_of(t * WIDE, WIDE), WIDE)
-        right = bpts[ref, :, cols]
-        for b in range(n_cen // TILE):
-            rows = pl.ds(b * TILE, TILE)
-            kts[ref][rows, cols] = jnp.exp2(dot(arow[rows, :], right)).astype(BF16)
+    def nm_cols(t):
+        return pl.ds(pl.multiple_of(t * WIDE, WIDE), WIDE)
 
     def nm_sum(t, ref):
-        cols = pl.ds(pl.multiple_of(t * WIDE, WIDE), WIDE)
-        fpart[ref, :, cols] = dot(w_ref[...], kts[ref][:, cols])
+        fpart[ref, :, nm_cols(t)] = dot(w_ref[...], kts[ref][:, nm_cols(t)])
 
     def nm_step(t, first):
-        if not first:
-            nm_sum(t - 1, 1)
-        nm_tiles(t, 0)
-        nm_sum(t, 0)
-        nm_tiles(t, 1)
+        for ref in range(2):
+            right = bpts[ref, :, nm_cols(t)]
+            acc = None
+            for b in range(n_cen // TILE):
+                rows = pl.ds(b * TILE, TILE)
+                if ref or not first:
+                    one = dot(w_ref[:, rows], kts[1 - ref][rows, nm_cols(t + ref - 1)])
+                    acc = one if acc is None else acc + one
+                kts[ref][rows, nm_cols(t)] = jnp.exp2(dot(arow[rows, :], right)).astype(BF16)
+            if ref or not first:
+                fpart[1 - ref, :, nm_cols(t + ref - 1)] = acc
 
     piece = cpts // 2
 
@@ -232,27 +233,30 @@
             ag(q, k).wait_recv()
         d2(q).start()
 
-    def mm_tiles(body, ref):
-        cols = slice(ref * WIDE, (ref + 1) * WIDE)
-        fill(zaug, zbuf[body, 0:feats, cols], scale, False, cols)
-        left = zaug[:, cols].T
-        for b in range(n_cen // TILE):
-            cols = pl.ds(b * TILE, TILE)
-            tiles[ref][:, cols] = jnp.exp2(dot(left, bown[:, cols])).astype(BF16)
-
-    def mm_sum(body, ref, first=False):
-        weights = zbuf[body, feats : feats + outs, ref * WIDE : (ref + 1) * WIDE]
-        for b in range(n_cen // TILE):
-            cols = pl.ds(b * TILE, TILE)
-            one = dot(weights, tiles[ref][:, cols])
-            mmacc[:, cols] = one if first else mmacc[:, cols] + one
+    hcen = n_cen // 2
+
+    def mm_sum(body, ref, b, acc):
+        rows = pl.ds(b * TILE, TILE)
+        one = dot(zbuf[body, feats : feats + outs, rows], tiles[ref][rows, :])
+        return one if acc is None else acc + one
+
+    def mm_add(ref, acc, first):
+        cols = slice(ref * hcen, (ref + 1) * hcen)
+        mmacc[:, cols] = acc if first else mmacc[:, cols] + acc
 
     def mm(body, first):
-        if not first:
-            mm_sum(body - 1, 1)
-        mm_tiles(body, 0)
-        mm_sum(body, 0, first)
-        mm_tiles(body, 1)
+        for h in range(2):
+            cols = slice(h * WIDE, (h + 1) * WIDE)
+            fill(zaug, zbuf[body, 0:feats, cols], scale, False, cols)
+        for ref in range(2):
+            acc = None
+            for b in range(hcen // TILE):
+                rows = pl.ds(b * TILE, TILE)
+                if ref or not first:
+                    acc = mm_sum(body + ref - 1, 1 - ref, b, acc)
+                tiles[ref][rows, :] = jnp.exp2(dot(zaug[:, rows].T, bown[:, ref * hcen : (ref + 1) * hcen])).astype(BF16)
+            if ref or not first:
+                mm_add(1 - ref, acc, first)
 
     def actions(n, table):
         for step, todo in table.items():
@@ -290,6 +294,7 @@
         arrived(0, 0)
         arrived(0, 1)
 
+    mmacc[:, hcen:] = jnp.zeros((outs, hcen), F32)
     with jax.named_scope("mm_0"):
         mm(0, True)
     with jax.named_scope("mm_0_act"):
@@ -303,10 +308,10 @@
 
     table = {
         1: [],
-        2: [(z_came, 5), (z_came, 6), (x_came, 3), (x_came, 4), (ag_go, 0)],
-        3: [],
-        4: [(z_came, 7), (x_came, 5), (x_came, 6), (ag_go, 1)],
-        5: [(d2_go, 0)],
+        2: [(z_came, 5), (z_came, 6)],
+        3: [(x_came, 3), (x_came, 4), (ag_go, 0)],
+        4: [(z_came, 7)],
+        5: [(x_came, 5), (x_came, 6), (ag_go, 1), (d2_go, 0)],
         6: [(x_came, 7), (d2_go, 1)],
     }
 
@@ -327,39 +332,55 @@
 
     lax.fori_loop(1, 8, mm_body, 0)
     with jax.named_scope("mm_end"):
-        mm_sum(7, 1)
+        acc = None
+        for b in range(hcen // TILE):
+            acc = mm_sum(7, 1, b, acc)
+        mm_add(1, acc, False)
     with jax.named_scope("d2_wait"):
         d2(0).wait_recv()
         d2(1).wait_recv()
 
-    def back(k):
-        rows = pl.ds(pl.multiple_of(dp_peer(k) * dshare, dshare), dshare)
+    hshare = dshare // 2
+
+    def slice_of(peer, h):
+        return pl.ds(pl.multiple_of(peer * dshare + h * hshare, hshare), hshare)
+
+    def back(k, h):
+        rows = slice_of(dp_peer(k), h)
         total = dot_nt(fwd[0], kta[rows, :]) + dot_nt(fwd[1], ktb[rows, :])
         return total * norm + mmacc[:, rows]
 
-    def ds_copy(k):
-        return remote(dsend.at[k], drecv.at[k], ds_send.at[k], ds_recv.at[k], at(dp_peer(k), c))
-
-    def back_step(k, _):
-        dsend[k] = back(k)
-        ds_copy(k).start()
-        return 0
-
-    with jax.named_scope("back"):
-        lax.fori_loop(1, 8, back_step, 0)
-    with jax.named_scope("back0_dswait"):
-        total = back(0)
+    def ds_copy(k, h):
+        return remote(dsend.at[k, h], drecv.at[k, h], ds_send.at[k, h], ds_recv.at[k, h], at(dp_peer(k), c))
+
+    def dg(k, h):
+        where = outt.at[:, slice_of(d, h)]
+        return remote(where, where, dg_send.at[k, h], dg_recv.at[k, h], at(dp_peer(k), c))
+
+    def back_half(h):
+        def step(k, _):
+            dsend[k, h] = back(k, h)
+            ds_copy(k, h).start()
+            return 0
+
+        lax.fori_loop(1, 8, step, 0)
+        dsend[0, h] = back(0, h)
+
+    def share_out(h):
+        total = dsend[0, h]
         for k in range(1, 8):
-            ds_copy(k).wait_recv()
-            total = total + drecv[k]
-    mine = pl.ds(pl.multiple_of(d * dshare, dshare), dshare)
-    outt[:, mine] = total
-
-    def dg(k):
-        return remote(outt.at[:, mine], outt.at[:, mine], dg_send.at[k], dg_recv.at[k], at(dp_peer(k), c))
-
-    for k in range(1, 8):
-        dg(k).start()
+            ds_copy(k, h).wait_recv()
+            total = total + drecv[k, h]
+        outt[:, slice_of(d, h)] = total
+        for k in range(1, 8):
+            dg(k, h).start()
+
+    for h in range(2):
+        with jax.named_scope(f"back_{h}"):
+            back_half(h)
+    for h in range(2):
+        with jax.named_scope(f"share_{h}"):
+            share_out(h)
 
     for slab in range(8):
         if slab:
@@ -373,14 +394,16 @@
         for k in range(1, 16):
             rs(q, k).wait_send()
             ag(q, k).wait_send()
-    for k in range(1, 8):
-        ds_copy(k).wait_send()
-    with jax.named_scope("dg_wait_out"):
+    for h in range(2):
         for k in range(1, 8):
-            dg(k).wait_recv()
+            ds_copy(k, h).wait_send()
+            with jax.named_scope(f"dg_{h}_{k}"):
+                dg(k, h).wait_recv()
+    with jax.named_scope("out"):
         out_ref[...] = outt[...]
-    for k in range(1, 8):
-        dg(k).wait_send()
+    for h in range(2):
+        for k in range(1, 8):
+            dg(k, h).wait_send()
 
 
 def solution(mesh):
@@ -404,8 +427,8 @@
                 pltpu.VMEM((n_cen, ROWS), BF16),
                 pltpu.VMEM((n_cen, n_pts // 2), BF16),
                 pltpu.VMEM((n_cen, n_pts // 2), BF16),
-                pltpu.VMEM((WIDE, n_cen), BF16),
-                pltpu.VMEM((WIDE, n_cen), BF16),
+                pltpu.VMEM((n_cen // 2, n_cen // 2), BF16),
+                pltpu.VMEM((n_cen // 2, n_cen // 2), BF16),
                 pltpu.VMEM((2, outs, n_pts // 2), F32),
                 pltpu.VMEM((8, feats + outs, n_cen // 2), BF16),
                 pltpu.VMEM((ROWS, n_cen // 2), BF16),
@@ -415,16 +438,16 @@
                 pltpu.VMEM((CHUNKS, outs // 2, cpts), BF16),
                 pltpu.VMEM((CHUNKS, outs // 2, cpts), BF16),
                 pltpu.VMEM((CHUNKS, 16, outs // 2, cpts // 16), BF16),
-                pltpu.VMEM((8, outs, n_cen // 8), F32),
-                pltpu.VMEM((8, outs, n_cen // 8), F32),
+                pltpu.VMEM((8, 2, outs, n_cen // 16), F32),
+                pltpu.VMEM((8, 2, outs, n_cen // 16), F32),
                 pltpu.VMEM((outs, n_cen), F32),
                 *[dma((8,))] * 8, dma((2,)),
                 dma((CHUNKS,)), dma((CHUNKS,)),
                 dma((CHUNKS, 16)), dma((CHUNKS, 16)),
                 dma((CHUNKS, 16)), dma((CHUNKS, 16)),
                 dma((CHUNKS,)), dma((CHUNKS,)),
-                dma((8,)), dma((8,)),
-                dma((8,)), dma((8,)),
+                dma((8, 2)), dma((8, 2)),
+                dma((8, 2)), dma((8, 2)),
             ],
             compiler_params=pltpu.CompilerParams(
                 collective_id=0, has_side_effects=True, vmem_limit_bytes=60 * 1024 * 1024

time: 63.5 us -> 64.3 us (1.013)
  the two profiles are of different devices: /device:TPU:1 before, /device:TPU:64 now
where the time goes in v6:
time: 64.3 us; the launch traced here: 64.2 us
  Pallas kernels  62.3 us (97%)
  local copies, waits for them, and re-layouts  1.87 us (3%)
    pallas_call x1, Pallas kernels, on_device(): pl.pallas_call(body, out_shape=jax.ShapeDtypeStruct((outs, n_cen), F32),...  62.3 us
    unnamed x1, local copies, waits for them, and re-layouts  1.87 us

profile of v6, /device:TPU:64, one launch (start us, length us, event | category | flops | bytes accessed | tf_op | source)
XLA Modules:
  0.0 64.2 jit_solution(3511470286307123171)
XLA Ops:
  0.0 62.3 %shard_map.37 = f32[64,2048]{1,0:T(8,128)} custom-call(bf16[32,4096]{1,0:T(8,128)(2,1)} %bitcast.5, bf16[32,2048]{1,0:T(8,128)(2,1)} %bitcast.7, bf16[64,2048]{1,0:T(8,128)(2,1)} %bitcast.6), custom_call_target="tpu_custom_call" | custom-call | tf_op jit(solution)/shard_map/pallas_call | solution.py:419
  62.3 1.9 %copy.5 = f32[2048,64]{0,1:T(8,128)} copy(f32[2048,64]{0,1:T(8,128)} %bitcast.4) | data formatting | bytes 1048576

commit v7 on v6

--- a/solution.py
+++ b/solution.py
@@ -52,7 +52,7 @@
 def kernel(
     feats, outs, n_pts, n_cen, total_pts,
     p_ref, c_ref, w_ref, out_ref,
-    bpts, bown, arow, kta, ktb, tilea, tileb, fpart, zbuf, zaug, mmacc, fwd,
+    bpts, bown, arow, kta, ktb, tilea, tileb, fpart, zbuf, zaug, zrow, mmacc, fwd,
     sbuf, dbuf, rsend, rrecv, dsend, drecv, outt,
     z_send, z_recv, x_send, x_recv, c1_send, c1_recv, c3_send, c3_recv, own_sem,
     d1_send, d1_recv, rs_send, rs_recv, ag_send, ag_recv,
@@ -248,13 +248,14 @@
         for h in range(2):
             cols = slice(h * WIDE, (h + 1) * WIDE)
             fill(zaug, zbuf[body, 0:feats, cols], scale, False, cols)
+            zrow[cols, :] = zaug[:, cols].T
         for ref in range(2):
             acc = None
             for b in range(hcen // TILE):
                 rows = pl.ds(b * TILE, TILE)
                 if ref or not first:
                     acc = mm_sum(body + ref - 1, 1 - ref, b, acc)
-                tiles[ref][rows, :] = jnp.exp2(dot(zaug[:, rows].T, bown[:, ref * hcen : (ref + 1) * hcen])).astype(BF16)
+                tiles[ref][rows, :] = jnp.exp2(dot(zrow[rows, :], bown[:, ref * hcen : (ref + 1) * hcen])).astype(BF16)
             if ref or not first:
                 mm_add(1 - ref, acc, first)
 
@@ -298,9 +299,9 @@
     with jax.named_scope("mm_0"):
         mm(0, True)
     with jax.named_scope("mm_0_act"):
-        rs_go(1)
         z_came(3)
         z_came(4)
+        rs_go(1)
         x_came(1)
         x_came(2)
         arrived(1, 0)
@@ -310,9 +311,9 @@
         1: [],
         2: [(z_came, 5), (z_came, 6)],
         3: [(x_came, 3), (x_came, 4), (ag_go, 0)],
-        4: [(z_came, 7)],
-        5: [(x_came, 5), (x_came, 6), (ag_go, 1), (d2_go, 0)],
-        6: [(x_came, 7), (d2_go, 1)],
+        4: [(z_came, 7), (ag_go, 1)],
+        5: [(x_came, 5), (x_came, 6)],
+        6: [(x_came, 7), (d2_go, 0)],
     }
 
     def mm_body(n, _):
@@ -331,6 +332,8 @@
         return 0
 
     lax.fori_loop(1, 8, mm_body, 0)
+    with jax.named_scope("d2_1"):
+        d2_go(1)
     with jax.named_scope("mm_end"):
         acc = None
         for b in range(hcen // TILE):
@@ -358,13 +361,18 @@
         return remote(where, where, dg_send.at[k, h], dg_recv.at[k, h], at(dp_peer(k), c))
 
     def back_half(h):
-        def step(k, _):
-            dsend[k, h] = back(k, h)
-            ds_copy(k, h).start()
+        def step(t, _):
+            for k in (2 * t + 1, 2 * t + 2):
+                dsend[k % 8, h] = back(k, h)
+            ds_copy(2 * t + 1, h).start()
+
+            @pl.when(t < 3)
+            def _():
+                ds_copy(2 * t + 2, h).start()
+
             return 0
 
-        lax.fori_loop(1, 8, step, 0)
-        dsend[0, h] = back(0, h)
+        lax.fori_loop(0, 4, step, 0)
 
     def share_out(h):
         total = dsend[0, h]
@@ -432,6 +440,7 @@
                 pltpu.VMEM((2, outs, n_pts // 2), F32),
                 pltpu.VMEM((8, feats + outs, n_cen // 2), BF16),
                 pltpu.VMEM((ROWS, n_cen // 2), BF16),
+                pltpu.VMEM((n_cen // 2, ROWS), BF16),
                 pltpu.VMEM((outs, n_cen), F32),
                 pltpu.VMEM((2, outs, n_pts // 2), BF16),
                 pltpu.VMEM((CHUNKS, outs // 2, cpts), BF16),
@@ -450,7 +459,7 @@
                 dma((8, 2)), dma((8, 2)),
             ],
             compiler_params=pltpu.CompilerParams(
-                collective_id=0, has_side_effects=True, vmem_limit_bytes=60 * 1024 * 1024
+                collective_id=0, has_side_effects=True, vmem_limit_bytes=40 * 1024 * 1024
             ),
         )(points.T, centers.T, coef.T).T
 

time: 64.3 us -> 60.1 us (0.935)
  the two profiles are of different devices: /device:TPU:64 before, /device:TPU:1 now
where the time goes in v7:
time: 60.1 us; the launch traced here: 60 us
  Pallas kernels  56.4 us (94%)
  local copies, waits for them, and re-layouts  3.6 us (6%)
    pallas_call x1, Pallas kernels, on_device(): pl.pallas_call(body, out_shape=jax.ShapeDtypeStruct((outs, n_cen), F32),...  56.4 us
    unnamed x7, local copies, waits for them, and re-layouts  3.6 us

profile of v7, /device:TPU:1, one launch (start us, length us, event | category | flops | bytes accessed | tf_op | source)
XLA Modules:
  0.0 60.0 jit_solution(11473659339317692633)
XLA Ops:
  0.0 0.0 copy-start
  0.0 0.9 %copy-done = bf16[4096,32]{0,1:T(8,128)(2,1)S(1)} copy-done((bf16[4096,32]{0,1:T(8,128)(2,1)S(1)}, bf16[4096,32]{0,1:T(8,128)(2,1)}, u32[]{:S(2)}) %copy-start) | copy-done | bytes 262168
  1.0 0.0 copy-start.1
  1.0 0.9 %copy-done.1 = bf16[2048,64]{0,1:T(8,128)(2,1)S(1)} copy-done((bf16[2048,64]{0,1:T(8,128)(2,1)S(1)}, bf16[2048,64]{0,1:T(8,128)(2,1)}, u32[]{:S(2)}) %copy-start.1) | copy-done | bytes 262168
  1.9 0.0 copy-start.2
  1.9 0.9 %copy-done.2 = bf16[2048,32]{0,1:T(8,128)(2,1)S(1)} copy-done((bf16[2048,32]{0,1:T(8,128)(2,1)S(1)}, bf16[2048,32]{0,1:T(8,128)(2,1)}, u32[]{:S(2)}) %copy-start.2) | copy-done | bytes 131096
  2.8 56.4 %shard_map.37 = f32[64,2048]{1,0:T(8,128)S(1)} custom-call(bf16[32,4096]{1,0:T(8,128)(2,1)S(1)} %bitcast.5, bf16[32,2048]{1,0:T(8,128)(2,1)S(1)} %bitcast.7, bf16[64,2048]{1,0:T(8,128)(2,1)S(1)} %bitcast.6), custom_call_target="tpu_custom_call" | custom-call | tf_op jit(solution)/shard_map/pallas_call | solution.py:427
  59.2 0.8 %copy.5 = f32[2048,64]{0,1:T(8,128)} copy(f32[2048,64]{0,1:T(8,128)S(1)} %bitcast.4) | data formatting | bytes 1048576
Async XLA Ops:
  0.0 0.9 %copy-start = (bf16[4096,32]{0,1:T(8,128)(2,1)S(1)}, bf16[4096,32]{0,1:T(8,128)(2,1)}, u32[]{:S(2)}) copy-start(bf16[4096,32]{0,1:T(8,128)(2,1)} %param.3) | copy-start | bytes 786436
  1.0 0.9 %copy-start.1 = (bf16[2048,64]{0,1:T(8,128)(2,1)S(1)}, bf16[2048,64]{0,1:T(8,128)(2,1)}, u32[]{:S(2)}) copy-start(bf16[2048,64]{0,1:T(8,128)(2,1)} %param.5) | copy-start | bytes 786436
  1.9 0.9 %copy-start.2 = (bf16[2048,32]{0,1:T(8,128)(2,1)S(1)}, bf16[2048,32]{0,1:T(8,128)(2,1)}, u32[]{:S(2)}) copy-start(bf16[2048,32]{0,1:T(8,128)(2,1)} %param.4) | copy-start | bytes 393220

commit v8 on v7

--- a/solution.py
+++ b/solution.py
@@ -51,10 +51,11 @@
 
 def kernel(
     feats, outs, n_pts, n_cen, total_pts,
-    p_ref, c_ref, w_ref, out_ref,
+    p_hbm, c_hbm, w_hbm, out_ref,
+    p_ref, c_ref, w_ref,
     bpts, bown, arow, kta, ktb, tilea, tileb, fpart, zbuf, zaug, zrow, mmacc, fwd,
     sbuf, dbuf, rsend, rrecv, dsend, drecv, outt,
-    z_send, z_recv, x_send, x_recv, c1_send, c1_recv, c3_send, c3_recv, own_sem,
+    z_send, z_recv, x_send, x_recv, c1_send, c1_recv, c3_send, c3_recv, own_sem, in_sem,
     d1_send, d1_recv, rs_send, rs_recv, ag_send, ag_recv,
     d2_send, d2_recv, ds_send, ds_recv, dg_send, dg_recv,
 ):
@@ -92,6 +93,13 @@
             src_ref=src, dst_ref=dst, send_sem=send, recv_sem=recv, device_id=dev, device_id_type=MESH
         )
 
+    fetch = [
+        pltpu.make_async_copy(src, dst, in_sem.at[n])
+        for n, (src, dst) in enumerate(((c_hbm, c_ref), (p_hbm, p_ref), (w_hbm, w_ref)))
+    ]
+    for copy in fetch:
+        copy.start()
+
     barrier = pltpu.get_barrier_semaphore()
     for k in range(1, 16):
         pl.semaphore_signal(barrier, inc=1, device_id=group(k), device_id_type=MESH)
@@ -112,7 +120,9 @@
         return 0
 
     with jax.named_scope("prep"):
+        fetch[0].wait()
         lax.fori_loop(0, n_cen // TILE, prep_own, 0)
+        fetch[1].wait()
         lax.fori_loop(0, n_pts // 1024, prep_pts, 0)
 
     part = n_cen // 8
@@ -159,7 +169,7 @@
 
     a_own = [
         pltpu.make_async_copy(src.at[:, own_part], zbuf.at[0, lo : lo + src.shape[0], 0:part], own_sem.at[n])
-        for n, (src, lo) in enumerate(((c_ref, 0), (w_ref, feats)))
+        for n, (src, lo) in enumerate(((c_hbm, 0), (w_hbm, feats)))
     ]
     for copy in a_own:
         copy.start()
@@ -268,6 +278,7 @@
                     f(q)
 
     steps = n_pts // WIDE // 2
+    fetch[2].wait()
     with jax.named_scope("nm_a"):
         nm_step(0, True)
     with jax.named_scope("barrier"):
@@ -309,11 +320,11 @@
 
     table = {
         1: [],
-        2: [(z_came, 5), (z_came, 6)],
-        3: [(x_came, 3), (x_came, 4), (ag_go, 0)],
-        4: [(z_came, 7), (ag_go, 1)],
-        5: [(x_came, 5), (x_came, 6)],
-        6: [(x_came, 7), (d2_go, 0)],
+        2: [(z_came, 5), (z_came, 6), (x_came, 3), (x_came, 4), (ag_go, 0)],
+        3: [(ag_go, 1)],
+        4: [(z_came, 7), (x_came, 5), (x_came, 6)],
+        5: [(x_came, 7), (d2_go, 0)],
+        6: [(d2_go, 1)],
     }
 
     def mm_body(n, _):
@@ -325,15 +336,15 @@
                 @pl.when(n == step)
                 def _():
                     for f, q in todo:
-                        f(q)
-                    arrived(step + 1, 0)
-                    arrived(step + 1, 1)
+                        with jax.named_scope(f"{f.__name__}_{q}"):
+                            f(q)
+                    with jax.named_scope(f"arrived_{step + 1}"):
+                        arrived(step + 1, 0)
+                        arrived(step + 1, 1)
 
         return 0
 
     lax.fori_loop(1, 8, mm_body, 0)
-    with jax.named_scope("d2_1"):
-        d2_go(1)
     with jax.named_scope("mm_end"):
         acc = None
         for b in range(hcen // TILE):
@@ -427,9 +438,12 @@
         return pl.pallas_call(
             body,
             out_shape=jax.ShapeDtypeStruct((outs, n_cen), F32),
-            in_specs=[pl.BlockSpec(memory_space=pltpu.VMEM)] * 3,
+            in_specs=[pl.BlockSpec(memory_space=pltpu.HBM)] * 3,
             out_specs=pl.BlockSpec(memory_space=pltpu.VMEM),
             scratch_shapes=[
+                pltpu.VMEM((feats, n_pts), BF16),
+                pltpu.VMEM((feats, n_cen), BF16),
+                pltpu.VMEM((outs, n_cen), BF16),
                 pltpu.VMEM((2, ROWS, n_pts // 2), BF16),
                 pltpu.VMEM((ROWS, n_cen), BF16),
                 pltpu.VMEM((n_cen, ROWS), BF16),
@@ -450,7 +464,7 @@
                 pltpu.VMEM((8, 2, outs, n_cen // 16), F32),
                 pltpu.VMEM((8, 2, outs, n_cen // 16), F32),
                 pltpu.VMEM((outs, n_cen), F32),
-                *[dma((8,))] * 8, dma((2,)),
+                *[dma((8,))] * 8, dma((2,)), dma((3,)),
                 dma((CHUNKS,)), dma((CHUNKS,)),
                 dma((CHUNKS, 16)), dma((CHUNKS, 16)),
                 dma((CHUNKS, 16)), dma((CHUNKS, 16)),
@@ -461,7 +475,7 @@
             compiler_params=pltpu.CompilerParams(
                 collective_id=0, has_side_effects=True, vmem_limit_bytes=40 * 1024 * 1024
             ),
-        )(points.T, centers.T, coef.T).T
+        )(*(pltpu.with_memory_space_constraint(a.T, pltpu.HBM) for a in (points, centers, coef))).T
 
     in_specs = (P("dp", None), P("centers", None), P("centers", None))
     return jax.shard_map(

time: 60.1 us -> 56.6 us (0.942); the launches traced: 60 us -> 55.6 us
  local copies, waits for them, and re-layouts: 3.6 us -> 0.8 us
  Pallas kernels: 56.4 us -> 54.8 us
    unnamed x7 -> x1, local copies, waits for them, and re-layouts: 3.6 us -> 0.8 us
    pallas_call x1, Pallas kernels: 56.4 us -> 54.8 us  [on_device(): pl.pallas_call(body, out_shape=jax.ShapeDtypeStruct((outs, n_cen), F32),...]
where the time goes in v8:
time: 56.6 us; the launch traced here: 55.6 us
  Pallas kernels  54.8 us (97%)
  local copies, waits for them, and re-layouts  0.8 us (1%)
    pallas_call x1, Pallas kernels, on_device(): pl.pallas_call(body, out_shape=jax.ShapeDtypeStruct((outs, n_cen), F32),...  54.8 us

profile of v8, /device:TPU:1, one launch (start us, length us, event | category | flops | bytes accessed | tf_op | source)
XLA Modules:
  0.0 55.6 jit_solution(6287144888018941513)
XLA Ops:
  0.0 54.8 %shard_map.37 = f32[64,2048]{1,0:T(8,128)S(1)} custom-call(bf16[32,4096]{1,0:T(8,128)(2,1)} %bitcast.5, bf16[32,2048]{1,0:T(8,128)(2,1)} %bitcast.7, bf16[64,2048]{1,0:T(8,128)(2,1)} %bitcast.6), custom_call_target="tpu_custom_call" | custom-call | tf_op jit(solution)/shard_map/pallas_call | solution.py:438
  54.8 0.8 %copy.5 = f32[2048,64]{0,1:T(8,128)} copy(f32[2048,64]{0,1:T(8,128)S(1)} %bitcast.4) | data formatting | bytes 1048576

commit v9 on v8

--- a/solution.py
+++ b/solution.py
@@ -78,6 +78,7 @@
 
     partner = at(d, chip * 2 + 1 - core)
     x_next = at(d, z * 4 + (1 - x_lo) * 2 + core)
+    x_cross = at(d, z * 4 + (1 - x_lo) * 2 + 1 - core)
 
     def chip_peer(k):
         return (chip + k) % 16
@@ -103,7 +104,8 @@
     barrier = pltpu.get_barrier_semaphore()
     for k in range(1, 16):
         pl.semaphore_signal(barrier, inc=1, device_id=group(k), device_id_type=MESH)
-    pl.semaphore_signal(barrier, inc=1, device_id=partner, device_id_type=MESH)
+    for peer in (partner, x_cross):
+        pl.semaphore_signal(barrier, inc=1, device_id=peer, device_id_type=MESH)
     for k in range(1, 8):
         pl.semaphore_signal(barrier, inc=1, device_id=at(dp_peer(k), c), device_id_type=MESH)
 
@@ -147,6 +149,8 @@
         return remote(place(slab, 0), place(slab, 1), c1_send.at[slab], c1_recv.at[slab], partner)
 
     def a_cross(slab):
+        if slab == 7:
+            return remote(place(7, 0), place(7, 3), c3_send.at[7], c3_recv.at[7], x_cross)
         return remote(place(slab, 2), place(slab, 3), c3_send.at[slab], c3_recv.at[slab], partner)
 
     def z_came(slab):
@@ -155,6 +159,8 @@
             a_z(slab + 2).start()
         a_core(slab).start()
         a_x(slab).start()
+        if slab == 7:
+            a_cross(slab).start()
 
     def x_came(slab):
         a_x(slab).wait_recv()
@@ -162,6 +168,8 @@
 
     def arrived(body, h):
         if body in (0, 7):
+            if body == 7 and h == 1:
+                a_x(7).wait_recv()
             (a_cross if h else a_core)(body).wait_recv()
         else:
             slab = (body - 1) // 2 * 2 + 1 + h
@@ -179,6 +187,9 @@
 
     def nm_sum(t, ref):
         fpart[ref, :, nm_cols(t)] = dot(w_ref[...], kts[ref][:, nm_cols(t)])
+
+    def nm_sum_b(t):
+        nm_sum(t, 1)
 
     def nm_step(t, first):
         for ref in range(2):
@@ -244,14 +255,15 @@
         d2(q).start()
 
     hcen = n_cen // 2
-
-    def mm_sum(body, ref, b, acc):
+    groups = n_cen // WIDE
+
+    def mm_sum(body, g, b, acc):
         rows = pl.ds(b * TILE, TILE)
-        one = dot(zbuf[body, feats : feats + outs, rows], tiles[ref][rows, :])
+        one = dot(zbuf[body, feats : feats + outs, rows], tiles[g % 2][rows, :])
         return one if acc is None else acc + one
 
-    def mm_add(ref, acc, first):
-        cols = slice(ref * hcen, (ref + 1) * hcen)
+    def mm_add(g, acc, first):
+        cols = slice(g * WIDE, (g + 1) * WIDE)
         mmacc[:, cols] = acc if first else mmacc[:, cols] + acc
 
     def mm(body, first):
@@ -259,15 +271,16 @@
             cols = slice(h * WIDE, (h + 1) * WIDE)
             fill(zaug, zbuf[body, 0:feats, cols], scale, False, cols)
             zrow[cols, :] = zaug[:, cols].T
-        for ref in range(2):
+        for g in range(groups):
             acc = None
+            last = (g - 1) % groups
             for b in range(hcen // TILE):
                 rows = pl.ds(b * TILE, TILE)
-                if ref or not first:
-                    acc = mm_sum(body + ref - 1, 1 - ref, b, acc)
-                tiles[ref][rows, :] = jnp.exp2(dot(zrow[rows, :], bown[:, ref * hcen : (ref + 1) * hcen])).astype(BF16)
-            if ref or not first:
-                mm_add(1 - ref, acc, first)
+                if g or not first:
+                    acc = mm_sum(body if g else body - 1, last, b, acc)
+                tiles[g % 2][rows, :] = jnp.exp2(dot(zrow[rows, :], bown[:, g * WIDE : (g + 1) * WIDE])).astype(BF16)
+            if g or not first:
+                mm_add(last, acc, first)
 
     def actions(n, table):
         for step, todo in table.items():
@@ -282,7 +295,7 @@
     with jax.named_scope("nm_a"):
         nm_step(0, True)
     with jax.named_scope("barrier"):
-        pl.semaphore_wait(barrier, 23)
+        pl.semaphore_wait(barrier, 24)
     for copy in a_own:
         copy.wait()
     a_z(1).start()
@@ -294,7 +307,7 @@
         with jax.named_scope("nm_body"):
             nm_step(n, False)
         with jax.named_scope("nm_act"):
-            actions(n, {2: [(d1_go, 0), (z_came, 1), (z_came, 2), (x_came, 0)]})
+            actions(n, {1: [(nm_sum_b, 1), (d1_go, 0)], 2: [(z_came, 1), (z_came, 2), (x_came, 0), (rs_go, 0)]})
         return 0
 
     lax.fori_loop(1, steps, nm_body, 0)
@@ -302,11 +315,10 @@
         nm_sum(steps - 1, 1)
     with jax.named_scope("nm_end_act"):
         d1_go(1)
-        rs_go(0)
         arrived(0, 0)
         arrived(0, 1)
 
-    mmacc[:, hcen:] = jnp.zeros((outs, hcen), F32)
+    mmacc[:, (groups - 1) * WIDE :] = jnp.zeros((outs, WIDE), F32)
     with jax.named_scope("mm_0"):
         mm(0, True)
     with jax.named_scope("mm_0_act"):
@@ -319,11 +331,11 @@
         arrived(1, 1)
 
     table = {
-        1: [],
-        2: [(z_came, 5), (z_came, 6), (x_came, 3), (x_came, 4), (ag_go, 0)],
+        1: [(ag_go, 0)],
+        2: [(z_came, 5), (z_came, 6), (x_came, 3), (x_came, 4)],
         3: [(ag_go, 1)],
         4: [(z_came, 7), (x_came, 5), (x_came, 6)],
-        5: [(x_came, 7), (d2_go, 0)],
+        5: [(d2_go, 0)],
         6: [(d2_go, 1)],
     }
 
@@ -348,8 +360,8 @@
     with jax.named_scope("mm_end"):
         acc = None
         for b in range(hcen // TILE):
-            acc = mm_sum(7, 1, b, acc)
-        mm_add(1, acc, False)
+            acc = mm_sum(7, groups - 1, b, acc)
+        mm_add(groups - 1, acc, False)
     with jax.named_scope("d2_wait"):
         d2(0).wait_recv()
         d2(1).wait_recv()
@@ -449,8 +461,8 @@
                 pltpu.VMEM((n_cen, ROWS), BF16),
                 pltpu.VMEM((n_cen, n_pts // 2), BF16),
                 pltpu.VMEM((n_cen, n_pts // 2), BF16),
-                pltpu.VMEM((n_cen // 2, n_cen // 2), BF16),
-                pltpu.VMEM((n_cen // 2, n_cen // 2), BF16),
+                pltpu.VMEM((n_cen // 2, WIDE), BF16),
+                pltpu.VMEM((n_cen // 2, WIDE), BF16),
                 pltpu.VMEM((2, outs, n_pts // 2), F32),
                 pltpu.VMEM((8, feats + outs, n_cen // 2), BF16),
                 pltpu.VMEM((ROWS, n_cen // 2), BF16),

time: 56.6 us -> 54.9 us (0.970); the launches traced: 55.6 us -> 54.6 us
  Pallas kernels: 54.8 us -> 53.8 us
    pallas_call x1, Pallas kernels: 54.8 us -> 53.8 us  [on_device(): pl.pallas_call(body, out_shape=jax.ShapeDtypeStruct((outs, n_cen), F32),...]
where the time goes in v9:
time: 54.9 us; the launch traced here: 54.6 us
  Pallas kernels  53.8 us (98%)
  local copies, waits for them, and re-layouts  0.8 us (1%)
    pallas_call x1, Pallas kernels, on_device(): pl.pallas_call(body, out_shape=jax.ShapeDtypeStruct((outs, n_cen), F32),...  53.8 us

profile of v9, /device:TPU:1, one launch (start us, length us, event | category | flops | bytes accessed | tf_op | source)
XLA Modules:
  0.0 54.6 jit_solution(9888022735244295024)
XLA Ops:
  0.0 53.8 %shard_map.37 = f32[64,2048]{1,0:T(8,128)S(1)} custom-call(bf16[32,4096]{1,0:T(8,128)(2,1)} %bitcast.5, bf16[32,2048]{1,0:T(8,128)(2,1)} %bitcast.7, bf16[64,2048]{1,0:T(8,128)(2,1)} %bitcast.6), custom_call_target="tpu_custom_call" | custom-call | tf_op jit(solution)/shard_map/pallas_call | solution.py:450
  53.8 0.8 %copy.5 = f32[2048,64]{0,1:T(8,128)} copy(f32[2048,64]{0,1:T(8,128)S(1)} %bitcast.4) | data formatting | bytes 1048576

commit v10 on v9

--- a/solution.py
+++ b/solution.py
@@ -14,6 +14,8 @@
 TILE = 256
 WIDE = 512
 CHUNKS = 2
+FAR_CHIPS = (8, 7, 9, 6, 10, 5, 11, 4, 12, 3, 13, 2, 14, 1, 15)
+FAR_PLANES = (3, 5, 1, 7, 4, 2, 6)
 
 
 def split3(x):
@@ -226,7 +228,7 @@
             lanes = slice(e * piece, (e + 1) * piece)
             mine = fpart[e, own_rows, q * piece : (q + 1) * piece]
             rsend[q, :, lanes] = (mine + dbuf[q, :, lanes].astype(F32)).astype(BF16)
-        for k in range(1, 16):
+        for k in FAR_CHIPS:
             rs(q, k).start()
 
     def own_share(q):
@@ -242,7 +244,7 @@
             rs(q, k).wait_recv()
             total = total + rrecv[q, k].astype(F32)
         fwd[own_share(q)] = total.astype(BF16)
-        for k in range(1, 16):
+        for k in FAR_CHIPS:
             ag(q, k).start()
 
     def d2(q):
@@ -403,7 +405,7 @@
             ds_copy(k, h).wait_recv()
             total = total + drecv[k, h]
         outt[:, slice_of(d, h)] = total
-        for k in range(1, 8):
+        for k in FAR_PLANES:
             dg(k, h).start()
 
     for h in range(2):

time: 54.9 us -> 55 us (level)
  no operation moved by 1% of the time
where the time goes in v10:
time: 55 us; the launch traced here: 54.5 us
  Pallas kernels  53.7 us (98%)
  local copies, waits for them, and re-layouts  0.8 us (1%)
    pallas_call x1, Pallas kernels, on_device(): pl.pallas_call(body, out_shape=jax.ShapeDtypeStruct((outs, n_cen), F32),...  53.7 us

profile of v10, /device:TPU:1, one launch (start us, length us, event | category | flops | bytes accessed | tf_op | source)
XLA Modules:
  0.0 54.5 jit_solution(13371109125849200372)
XLA Ops:
  0.0 53.7 %shard_map.37 = f32[64,2048]{1,0:T(8,128)S(1)} custom-call(bf16[32,4096]{1,0:T(8,128)(2,1)} %bitcast.5, bf16[32,2048]{1,0:T(8,128)(2,1)} %bitcast.7, bf16[64,2048]{1,0:T(8,128)(2,1)} %bitcast.6), custom_call_target="tpu_custom_call" | custom-call | tf_op jit(solution)/shard_map/pallas_call | solution.py:452
  53.7 0.8 %copy.5 = f32[2048,64]{0,1:T(8,128)} copy(f32[2048,64]{0,1:T(8,128)S(1)} %bitcast.4) | data formatting | bytes 1048576
